TPU v7x, 128 devices: a whole 4x4x4 slice. The times are simulated.
128 devices in a mesh: leaf: 16 (over y, z_hi, core), seq: 8 (over z_lo, x).
Axes of the slice: x: 4, y: 4, z: 4 (z_hi: 2, z_lo: 2; z = z_hi * 2 + z_lo), core: 2. Of those that a mesh axis runs over, the one named last changes fastest.
Arguments:
- prompt_q: bfloat16 [16, 1024, 1792], P('leaf', 'seq'), may hold values from -6 to 6
- prompt_k: bfloat16 [16, 1024, 256], P('leaf', 'seq'), may hold values from -6 to 6
- prompt_value_rows: bfloat16 [16, 1024, 256], P('leaf', 'seq'), may hold values from -6 to 6
- leaf_q: bfloat16 [16, 384, 1792], P('leaf', 'seq'), may hold values from -6 to 6
- leaf_k: bfloat16 [16, 384, 256], P('leaf', 'seq'), may hold values from -6 to 6
- leaf_value_rows: bfloat16 [16, 384, 256], P('leaf', 'seq'), may hold values from -6 to 6
- prompt_dy: bfloat16 [16, 1024, 3584], P('leaf', 'seq'), may hold values from -6 to 6
- leaf_dy: bfloat16 [16, 384, 3584], P('leaf', 'seq'), may hold values from -6 to 6
- out_weight: bfloat16 [1792, 3584], replicated, may hold values from -0.125 to 0.125
- lengths: int32 [16, 16], P('leaf'), may hold values from 1 to 48, 384 in all within a row
- offsets: int32 [16, 16], P('leaf'), may hold values from 1 to 1024
- parents: int32 [16, 16], P('leaf'), may hold values from 0 to 15, as said below
Outputs:
- prompt_dq: float32 [16, 1024, 1792], P('leaf', 'seq')
- prompt_dk: float32 [16, 1024, 256], P('leaf', 'seq')
- prompt_dv: float32 [16, 1024, 256], P('leaf', 'seq')
- leaf_dq: float32 [16, 384, 1792], P('leaf', 'seq')
- leaf_dk: float32 [16, 384, 256], P('leaf', 'seq')
- leaf_dv: float32 [16, 384, 256], P('leaf', 'seq')
- weight_grad: float32 [1792, 3584], P(('leaf', 'seq'))
Inputs may be any that keep to these rules, and one draw needn't show every extreme that they name: parents[t, b] lies in 0 to b; the value b means that branch b has no ancestor branch.
All inputs are finite; a program needn't handle non-finite values.
Results may differ from a plain program's by a relative error of at most 0.025.
Values may be sent and summed in bfloat16 or wider, within the bound.
A program may use at most 128 MiB of HBM per device.

v0:
```python
import math

import jax
import jax.numpy as jnp
from jax import lax
from jax.sharding import PartitionSpec as P

HEAD_SIZE = 128
QUERY_HEADS = 14
KEY_VALUE_HEADS = 2
QUERY_PER_KV = 7


def cut_along(value, dim, peers):
    before, after = (value.shape[:dim], value.shape[dim + 1 :])
    return jnp.moveaxis(value.reshape(*before, peers, -1, *after), dim, 0)


def sum_at_owner(value, axis, dim):
    peers = lax.axis_size(axis)
    pieces = lax.all_to_all(cut_along(value, dim, peers), axis, 0, 0, tiled=True)
    return jnp.sum(pieces.astype(jnp.float32), axis=0)


def side_by_side(arrays, axis, dim, along):
    widths = [a.shape[along] for a in arrays]
    both = jnp.concatenate(arrays, axis=along)
    filled = lax.all_gather(both, axis, axis=dim, tiled=True)
    return tuple(jnp.split(filled, [sum(widths[:k]) for k in range(1, len(widths))], axis=along))


def leaf_visibility(lengths, offsets, parents, query_index, prompt_total, leaf_total):
    branch_ends = jnp.cumsum(lengths)
    branch_ids = jnp.arange(lengths.shape[0], dtype=jnp.int32)
    leaf_index = jnp.arange(leaf_total, dtype=jnp.int32)
    key_branch = jnp.sum((leaf_index[:, None] >= branch_ends[None, :]).astype(jnp.int32), axis=1)
    query_branch = jnp.sum((query_index[:, None] >= branch_ends[None, :]).astype(jnp.int32), axis=1)
    member = (query_branch[:, None] == branch_ids[None, :]).astype(jnp.int32)
    fork_point = jnp.sum(member * offsets[None, :], axis=1)
    ancestor = jnp.sum(member * parents[None, :], axis=1)
    prompt_index = jnp.arange(prompt_total, dtype=jnp.int32)
    sees_prompt = prompt_index[None, :] < fork_point[:, None]
    own_branch = (key_branch[None, :] == query_branch[:, None]) & (
        leaf_index[None, :] <= query_index[:, None]
    )
    inherited = (key_branch[None, :] == ancestor[:, None]) & (
        ancestor[:, None] != query_branch[:, None]
    )
    return jnp.concatenate([sees_prompt, own_branch | inherited], axis=1)


def weight_gradient(attn_out, upstream, tree_count, seq_count):
    width_total = attn_out.shape[1]
    device_rows = attn_out.shape[0]
    row_share = width_total // (tree_count * seq_count)
    normalizer = 1.0 / math.sqrt(tree_count * seq_count * device_rows)
    parted = attn_out.reshape(device_rows, tree_count, seq_count, row_share)
    moved = lax.all_to_all(parted, "seq", split_axis=2, concat_axis=0, tiled=True)
    picked = moved.reshape(device_rows * seq_count, tree_count * row_share)
    tree_grad = lax.all_gather(upstream, "seq", axis=0, tiled=True)
    partial_term = lax.dot_general(
        picked, tree_grad, (((0,), (0,)), ((), ())), preferred_element_type=jnp.float32
    )
    summed = sum_at_owner(partial_term.astype(jnp.bfloat16), "leaf", 0)
    return summed * normalizer


def body(
    prompt_q,
    prompt_k,
    prompt_value_rows,
    leaf_q,
    leaf_k,
    leaf_value_rows,
    prompt_dy,
    leaf_dy,
    out_weight,
    lengths,
    offsets,
    parents,
):
    seq_count = lax.axis_size("seq")
    tree_count = lax.axis_size("leaf")
    seq_index = lax.axis_index("seq")
    prompt_dev = prompt_q.shape[1]
    leaf_dev = leaf_q.shape[1]
    device_rows = prompt_dev + leaf_dev
    prompt_total = prompt_dev * seq_count
    leaf_total = leaf_dev * seq_count
    score_scale = 1.0 / math.sqrt(HEAD_SIZE)
    gathered = (
        *side_by_side((prompt_k, prompt_value_rows), "seq", 1, 0),
        *side_by_side((leaf_k, leaf_value_rows), "seq", 1, 0),
    )
    key_rows = jnp.concatenate([gathered[0][0], gathered[2][0]], axis=0)
    value_rows = jnp.concatenate([gathered[1][0], gathered[3][0]], axis=0)
    query_rows = jnp.concatenate([prompt_q[0], leaf_q[0]], axis=0)
    upstream = jnp.concatenate([prompt_dy[0], leaf_dy[0]], axis=0)
    prompt_index = seq_index * prompt_dev + jnp.arange(prompt_dev, dtype=jnp.int32)
    leaf_index = seq_index * leaf_dev + jnp.arange(leaf_dev, dtype=jnp.int32)
    prompt_keys = jnp.arange(prompt_total, dtype=jnp.int32)
    prompt_sees = jnp.concatenate(
        [
            prompt_keys[None, :] <= prompt_index[:, None],
            jnp.zeros((prompt_dev, leaf_total), dtype=jnp.bool_),
        ],
        axis=1,
    )
    leaf_sees = leaf_visibility(
        lengths[0], offsets[0], parents[0], leaf_index, prompt_total, leaf_total
    )
    visible = jnp.concatenate([prompt_sees, leaf_sees], axis=0)
    grouped_queries = query_rows.reshape(device_rows, KEY_VALUE_HEADS, QUERY_PER_KV, HEAD_SIZE)
    output_gradient = lax.dot_general(
        upstream, out_weight, (((1,), (1,)), ((), ())), preferred_element_type=jnp.float32
    ).astype(jnp.bfloat16)
    gradient_groups = output_gradient.reshape(device_rows, KEY_VALUE_HEADS, QUERY_PER_KV, HEAD_SIZE)
    prob_list, weight_list, attn_list = ([], [], [])
    for key_value_group in range(KEY_VALUE_HEADS):
        key_block = key_rows[:, key_value_group * HEAD_SIZE : (key_value_group + 1) * HEAD_SIZE]
        value_block = value_rows[:, key_value_group * HEAD_SIZE : (key_value_group + 1) * HEAD_SIZE]
        scores = (
            jnp.einsum(
                "qhd,kd->hqk",
                grouped_queries[:, key_value_group],
                key_block,
                preferred_element_type=jnp.float32,
            )
            * score_scale
        )
        scores = jnp.where(visible[None], scores, -jnp.inf)
        shifted = jnp.exp(scores - jnp.max(scores, axis=2, keepdims=True))
        probabilities = shifted / jnp.sum(shifted, axis=2, keepdims=True)
        weights = probabilities.astype(jnp.bfloat16)
        attn_list.append(
            jnp.einsum(
                "hqk,kd->qhd", weights, value_block, preferred_element_type=jnp.float32
            ).astype(jnp.bfloat16)
        )
        prob_list.append(probabilities)
        weight_list.append(weights)
    attn_out = jnp.stack(attn_list, axis=1).reshape(device_rows, QUERY_HEADS * HEAD_SIZE)
    dscore_list, dq_list = ([], [])
    for key_value_group in range(KEY_VALUE_HEADS):
        key_block = key_rows[:, key_value_group * HEAD_SIZE : (key_value_group + 1) * HEAD_SIZE]
        value_block = value_rows[:, key_value_group * HEAD_SIZE : (key_value_group + 1) * HEAD_SIZE]
        row_dot = jnp.sum(
            gradient_groups[:, key_value_group].astype(jnp.float32)
            * attn_list[key_value_group].astype(jnp.float32),
            axis=2,
        )
        prob_grad = jnp.einsum(
            "qhd,kd->hqk",
            gradient_groups[:, key_value_group],
            value_block,
            preferred_element_type=jnp.float32,
        )
        dscore = (
            prob_list[key_value_group] * (prob_grad - row_dot.T[:, :, None]) * score_scale
        ).astype(jnp.bfloat16)
        dq_list.append(
            jnp.einsum("hqk,kd->qhd", dscore, key_block, preferred_element_type=jnp.float32)
        )
        dscore_list.append(dscore)
    query_grad = jnp.stack(dq_list, axis=1).reshape(device_rows, QUERY_HEADS * HEAD_SIZE)
    first_block = jnp.int32(0) // device_rows
    blocks = device_rows * lax.axis_size("seq") // device_rows
    prompt_cols = blocks * prompt_dev
    leaf_cols = blocks * leaf_dev
    key_parts = []
    value_parts = []
    for key_value_group in range(KEY_VALUE_HEADS):
        picked_d = jnp.concatenate(
            [
                lax.dynamic_slice_in_dim(
                    dscore_list[key_value_group], first_block * prompt_dev, prompt_cols, 2
                ),
                lax.dynamic_slice_in_dim(dscore_list[key_value_group], prompt_total, leaf_cols, 2),
            ],
            axis=2,
        )
        picked_w = jnp.concatenate(
            [
                lax.dynamic_slice_in_dim(
                    weight_list[key_value_group], first_block * prompt_dev, prompt_cols, 2
                ),
                lax.dynamic_slice_in_dim(weight_list[key_value_group], prompt_total, leaf_cols, 2),
            ],
            axis=2,
        )
        key_parts.append(
            jnp.einsum(
                "hqk,qhd->kd",
                picked_d,
                grouped_queries[:, key_value_group],
                preferred_element_type=jnp.float32,
            )
        )
        value_parts.append(
            jnp.einsum(
                "hqk,qhd->kd",
                picked_w,
                gradient_groups[:, key_value_group],
                preferred_element_type=jnp.float32,
            )
        )
    joined = jnp.concatenate(key_parts + value_parts, axis=1)
    stacked_width = joined.shape[1]
    prompt_part = joined[:prompt_cols].reshape(blocks, prompt_dev, stacked_width)
    leaf_part = joined[prompt_cols:].reshape(blocks, leaf_dev, stacked_width)
    key_grads = sum_at_owner(
        jnp.concatenate([prompt_part, leaf_part], axis=1)
        .reshape(device_rows * lax.axis_size("seq"), stacked_width)
        .astype(jnp.bfloat16),
        "seq",
        0,
    )
    weight_grad = weight_gradient(attn_out, upstream, tree_count, seq_count)
    key_value_width = KEY_VALUE_HEADS * HEAD_SIZE
    return (
        query_grad[:prompt_dev][None],
        key_grads[:prompt_dev, :key_value_width][None],
        key_grads[:prompt_dev, key_value_width:][None],
        query_grad[prompt_dev:][None],
        key_grads[prompt_dev:, :key_value_width][None],
        key_grads[prompt_dev:, key_value_width:][None],
        weight_grad,
    )


def solution(mesh):
    placed = (
        P("leaf", "seq", None),
        P("leaf", "seq", None),
        P("leaf", "seq", None),
        P("leaf", "seq", None),
        P("leaf", "seq", None),
        P("leaf", "seq", None),
        P("leaf", "seq", None),
        P("leaf", "seq", None),
        P(),
        P("leaf", None),
        P("leaf", None),
        P("leaf", None),
    )
    return jax.shard_map(
        body,
        mesh=mesh,
        in_specs=placed,
        out_specs=(
            P("leaf", "seq", None),
            P("leaf", "seq", None),
            P("leaf", "seq", None),
            P("leaf", "seq", None),
            P("leaf", "seq", None),
            P("leaf", "seq", None),
            P(("leaf", "seq"), None),
        ),
        check_vma=False,
    )
```

profile of v0, /device:TPU:0, one launch (start us, length us, event | category | flops | bytes accessed | tf_op | source)
XLA Modules:
  0.0 236.4 jit_solution(1457289285222344115)
XLA Ops:
  7.2 1.6 pad_maximum_fusion.7
  8.9 2.4 %pad_maximum_fusion.1 = bf16[176,3584]{1,0:T(8,128)(2,1)} fusion(bf16[48,3584]{1,0:T(8,128)(2,1)} %bitcast.169, bf16[128,3584]{1,0:T(8,128)(2,1)} %bitcast.163), kind=kLoop, calls=%fused_computation.38 | loop fusion | flops 2523136 | bytes 2523136 | tf_op jit(solution)/shard_map/concatenate | solution.py:98
  11.5 9.0 %convolution_convert_fusion.1 = bf16[176,1792]{1,0:T(8,128)(2,1)S(1)} fusion(bf16[1792,3584]{1,0:T(8,128)(2,1)} %param.20, bf16[48,3584]{1,0:T(8,128)(2,1)S(1)} %bitcast.170, bf16[128,3584]{1,0:T(8,128)(2,1)S(1)} %bitcast.164), kind=kOutput, calls=%fused_computation.30 | convolution fusion | flops 2263568384 | bytes 14737408 | tf_op jit(solution)/shard_map/dot_general | solution.py:114
  20.5 0.7 reshape.95
  21.7 0.3 copy.55
  21.9 0.3 copy.56
  22.2 0.2 concatenate.50
  22.7 29.9 %all_gather.10 = bf16[2,384,256]{2,1,0:T(8,128)(2,1)S(1)} all-gather(bf16[2,48,256]{2,1,0:T(8,128)(2,1)S(1)} %pad_maximum_fusion.8), channel_id=1, replica_groups=mesh['leaf'=16,'seq'=8] {'seq'}, dimensions={1}, use_global_device_ids=true | all-gather | bytes 442368 | tf_op jit(solution)/shard_map/all_gather | solution.py:28
  52.9 0.7 slice_bitcast_fusion.2
  53.7 0.9 fusion.62
  54.6 2.1 slice_bitcast_fusion
  56.7 5.3 %fusion.70 = (f32[7,176]{1,0:T(8,128)S(1)}, f32[7,176,1408]{2,1,0:T(8,128)}) fusion(pred[176,1408]{1,0:T(8,128)(4,1)S(1)} %pad_add_fusion, bf16[48,2,7,128]{3,0,2,1:T(8,128)(2,1)S(1)} %copy.57, bf16[128,2,7,128]{3,0,2,1:T(8,128)(2,1)S(1)} %copy.56, bf16[384,256]{1,0:T(8,128)(2,1)S(1)} %get-tuple-element.35, bf16[1024,256]{1,0:T(8,128)(2,1)S(1)} %get-tuple-element.31), kind=kOutput, calls=%fused_computation.104 | convolution fusion | flops 452363648 | bytes 8543040 | tf_op jit(solution)/shard_map/sub | solution.py:132
  62.0 3.8 %fusion.17 = bf16[7,176,1408]{2,1,0:T(8,128)(2,1)S(1)} fusion(f32[7,176,1408]{2,1,0:T(8,128)} %get-tuple-element.45, f32[7,176]{1,0:T(8,128)S(1)} %get-tuple-element.44), kind=kLoop, calls=%fused_computation.29 | loop fusion | flops 3469312 | bytes 10412864 | tf_op jit(solution)/shard_map/convert_element_type | solution.py:134
  65.9 1.8 multiply_reduce_fusion
  67.7 6.5 %fusion.65 = (f32[7,176]{1,0:T(8,128)S(1)}, f32[7,176,1408]{2,1,0:T(8,128)}) fusion(pred[176,1408]{1,0:T(8,128)(4,1)} %copy-done.29, bf16[1024,256]{1,0:T(8,128)(2,1)} %copy-done.4, bf16[384,256]{1,0:T(8,128)(2,1)} %copy-done.12, bf16[128,2,7,128]{3,0,2,1:T(8,128)(2,1)} %copy-done.26, bf16[48,2,7,128]{3,0,2,1:T(8,128)(2,1)} %copy-done.31), kind=kOutput, calls=%fused_computation.103 | convolution fusion | flops 452363648 | bytes 8543040 | tf_op jit(solution)/shard_map/sub | solution.py:132
  74.2 3.8 %fusion.16 = bf16[7,176,1408]{2,1,0:T(8,128)(2,1)S(1)} fusion(f32[7,176,1408]{2,1,0:T(8,128)} %get-tuple-element.41, f32[7,176]{1,0:T(8,128)S(1)} %get-tuple-element.40), kind=kLoop, calls=%fused_computation.28 | loop fusion | flops 3469312 | bytes 10412864 | tf_op jit(solution)/shard_map/convert_element_type | solution.py:134
  78.0 1.8 copy-done
  79.9 1.2 multiply_reduce_fusion.1
  81.1 0.9 pad_maximum_fusion.2
  82.1 2.3 copy.65
  84.4 2.4 reshape_reshape.3
  86.7 2.7 %copy.66 = bf16[176,16,8,14]{0,1,3,2:T(8,128)(2,1)} copy(bf16[176,16,8,14]{0,3,2,1:T(8,128)(2,1)} %reshape_reshape.3) | data formatting | bytes 1261568 | tf_op jit(solution)/shard_map/reshape;reshape | solution.py:57
  89.4 5.0 %all-to-all-start.1 = ((bf16[176,16,8,14]{0,1,3,2:T(8,128)(2,1)}), bf16[176,16,8,14]{0,1,3,2:T(8,128)(2,1)}, u32[]{:S(2)}, u32[]{:S(2)}) async-start(bf16[176,16,8,14]{0,1,3,2:T(8,128)(2,1)} %copy.66), calls=%async_computation.1 | async-start | bytes 1835008 | tf_op jit(solution)/shard_map/all_to_all | solution.py:58
  94.5 1.9 convolution_bitcast_fusion
  96.3 0.2 copy-done.1
  96.6 0.7 convolution_bitcast_fusion.1
  97.4 0.4 copy-done.8
  97.8 4.5 %fusion.7 = bf16[7,176,1408]{2,1,0:T(8,128)(2,1)S(1)} fusion(f32[7,176]{1,0:T(8,128)S(1)} %bitcast.172, f32[7,176,1408]{2,1,0:T(8,128)} %get-tuple-element.41, f32[7,176]{1,0:T(8,128)S(1)} %get-tuple-element.40, bf16[176,1,7,128]{3,2,1,0:T(8,128)(2,1)S(1)} %copy-done.22, bf16[1024,256]{1,0:T(8,128)(2,1)S(1)} %copy-done.8, bf16[384,256]{1,0:T(8,128)(2,1)S(1)} %copy-done.16), kind=kOutput, calls=%fused_computation.10 | convolution fusion | flops 453466112 | bytes 11454080 | tf_op jit(solution)/shard_map/qhd,kd->hqk/dot_general | solution.py:152
  102.4 0.7 convolution_bitcast_fusion.3
  103.2 0.5 copy-done.20
  103.7 1.7 fusion.4
  105.4 0.7 convolution_bitcast_fusion.2
  106.2 1.1 copy-done.11
  107.3 0.2 copy.61
  107.5 1.1 maximum_convert_fusion
  108.8 0.5 copy.73
  109.3 1.2 pad_maximum_fusion
  110.5 3.1 %all-to-all-done.1 = bf16[176,16,8,14]{0,1,3,2:T(8,128)(2,1)} async-done(((bf16[176,16,8,14]{0,1,3,2:T(8,128)(2,1)}), bf16[176,16,8,14]{0,1,3,2:T(8,128)(2,1)}, u32[]{:S(2)}, u32[]{:S(2)}) %all-to-all-start.1) | async-done | bytes 630816 | tf_op jit(solution)/shard_map/all_to_all | solution.py:58
  113.6 7.1 %all-to-all-start = ((bf16[8,176,512]{2,1,0:T(8,128)(2,1)}), bf16[8,176,512]{2,1,0:T(8,128)(2,1)S(1)}, u32[]{:S(2)}, u32[]{:S(2)}) async-start(bf16[8,176,512]{2,1,0:T(8,128)(2,1)} %pad_maximum_fusion), calls=%async_computation | async-start | bytes 2883584 | tf_op jit(solution)/shard_map/all_to_all | solution.py:21
  120.8 1.7 copy.67
  122.5 1.8 reshape.98
  124.3 62.9 %all-gather.5.cloned.1.call-done = bf16[1408,3584]{1,0:T(8,128)(2,1)} async-done(((bf16[176,3584]{1,0:T(8,128)(2,1)}), bf16[1408,3584]{1,0:T(8,128)(2,1)}) %all-gather.5.cloned.1.call-update) | async-done | bytes 10092560 | tf_op jit(solution)/shard_map/all_gather | solution.py:60
  187.1 6.7 %convolution_convert_fusion = bf16[224,3584]{1,0:T(8,128)(2,1)S(1)} fusion(bf16[1408,224]{0,1:T(8,128)(2,1)} %reshape.98, bf16[1408,3584]{1,0:T(8,128)(2,1)} %all-gather.5.cloned.1.call-done), kind=kOutput, calls=%fused_computation.16 | convolution fusion | flops 2261532672 | bytes 12328960 | tf_op jit(solution)/shard_map/dot_general | solution.py:61
  193.9 1.5 reshape.99
  195.3 6.9 %all-to-all-start.2 = ((bf16[16,14,3584]{2,1,0:T(8,128)(2,1)}), bf16[16,14,3584]{2,1,0:T(8,128)(2,1)S(1)}, u32[]{:S(2)}, u32[]{:S(2)}) async-start(bf16[16,14,3584]{2,1,0:T(8,128)(2,1)} %reshape.99), calls=%async_computation.2 | async-start | bytes 3670016 | tf_op jit(solution)/shard_map/all_to_all | solution.py:21
  202.2 3.3 %convolution_bitcast_fusion.4 = f32[176,1,7,128]{3,0,2,1:T(8,128)S(1)} fusion(bf16[7,176,1408]{2,1,0:T(8,128)(2,1)} %copy-done.11, bf16[384,256]{1,0:T(8,128)(2,1)S(1)} %copy-done.13, bf16[1024,256]{1,0:T(8,128)(2,1)} %copy-done.4), kind=kOutput, calls=%fused_computation.36 | convolution fusion | flops 444792832 | bytes 4820992 | tf_op jit(solution)/shard_map/hqk,kd->qhd/dot_general | solution.py:162
  205.6 1.1 convolution_bitcast_fusion.5
  206.7 0.8 copy-done.3
  207.5 1.0 fusion.22
  208.5 2.4 %copy.60 = f32[128,2,7,128]{0,3,2,1:T(8,128)} copy(f32[128,2,7,128]{3,0,2,1:T(8,128)} %fusion.22) | data formatting | bytes 1835008 | tf_op jit(solution)/shard_map/slice | solution.py:221
  211.0 2.4 %copy.68 = f32[1,128,1792]{2,1,0:T(8,128)} copy(f32[1,128,1792]{1,2,0:T(8,128)} %bitcast.158) | data formatting | bytes 1835008
  213.4 1.0 pad_maximum_fusion.5
  214.4 0.9 copy.64
  215.3 1.8 broadcast_in_dim.33
  217.1 0.2 convert_reduce_fusion.1
  217.3 0.7 copy-done.17
  218.1 0.8 copy.69
  219.0 0.8 copy.70
  219.7 0.8 fusion.63
  220.7 0.7 copy.71
  221.5 0.7 copy.72
  222.2 6.4 %all-to-all-done.2 = bf16[16,14,3584]{2,1,0:T(8,128)(2,1)S(1)} async-done(((bf16[16,14,3584]{2,1,0:T(8,128)(2,1)}), bf16[16,14,3584]{2,1,0:T(8,128)(2,1)S(1)}, u32[]{:S(2)}, u32[]{:S(2)}) %all-to-all-start.2) | async-done | bytes 1605664 | tf_op jit(solution)/shard_map/all_to_all | solution.py:21
  228.6 0.3 convert_reduce_fusion
  228.9 0.7 broadcast_multiply_fusion
  (102 shorter events, 1.9 us)
Async XLA Ops:
  7.2 4.2 %copy-start.28 = (bf16[1,48,3584]{2,1,0:T(8,128)(2,1)S(1)}, bf16[1,48,3584]{2,1,0:T(8,128)(2,1)}, u32[]{:S(2)}) copy-start(bf16[1,48,3584]{2,1,0:T(8,128)(2,1)} %param.19) | copy-start | bytes 1032196
  7.2 4.2 %copy-start.24 = (bf16[1,128,3584]{2,1,0:T(8,128)(2,1)S(1)}, bf16[1,128,3584]{2,1,0:T(8,128)(2,1)}, u32[]{:S(2)}) copy-start(bf16[1,128,3584]{2,1,0:T(8,128)(2,1)} %param.18) | copy-start | bytes 2752516
  7.2 47.4 %all-gather.3.cloned.1.call-start = ((), (), s32[]{:S(2)}) async-start(), calls=%async_computation.3 | async-start | bytes 1179648 | tf_op jit(solution)/shard_map/all_gather | solution.py:28
  8.9 178.2 %all-gather.5.cloned.1.call-start = ((), (), s32[]{:S(2)}) async-start(), calls=%async_computation.4 | async-start | bytes 11354112 | tf_op jit(solution)/shard_map/all_gather | solution.py:60
  11.4 9.8 %copy-start.35 = (s32[1,16]{1,0:T(1,128)S(1)}, s32[1,16]{1,0:T(1,128)}, u32[]{:S(2)}) copy-start(s32[1,16]{1,0:T(1,128)} %param.21) | copy-start | bytes 196
  11.4 10.1 %copy-start.36 = (s32[1,16]{1,0:T(1,128)S(1)}, s32[1,16]{1,0:T(1,128)}, u32[]{:S(2)}) copy-start(s32[1,16]{1,0:T(1,128)} %param.22) | copy-start | bytes 196
  11.4 10.1 %copy-start.37 = (s32[1,16]{1,0:T(1,128)S(1)}, s32[1,16]{1,0:T(1,128)}, u32[]{:S(2)}) copy-start(s32[1,16]{1,0:T(1,128)} %param.23) | copy-start | bytes 196
  11.4 10.2 %copy-start.25 = (bf16[1,128,1792]{2,1,0:T(8,128)(2,1)S(1)}, bf16[1,128,1792]{2,1,0:T(8,128)(2,1)}, u32[]{:S(2)}) copy-start(bf16[1,128,1792]{2,1,0:T(8,128)(2,1)} %param.12) | copy-start | bytes 1376260
  11.4 10.8 %copy-start.30 = (bf16[1,48,1792]{2,1,0:T(8,128)(2,1)S(1)}, bf16[1,48,1792]{2,1,0:T(8,128)(2,1)}, u32[]{:S(2)}) copy-start(bf16[1,48,1792]{2,1,0:T(8,128)(2,1)} %param.15) | copy-start | bytes 516100
  20.5 2.1 copy-start.33
  20.5 2.1 copy-start.34
  22.2 39.8 %copy-start.26 = (bf16[128,2,7,128]{3,0,2,1:T(8,128)(2,1)}, bf16[128,2,7,128]{3,0,2,1:T(8,128)(2,1)S(1)}, u32[]{:S(2)}) copy-start(bf16[128,2,7,128]{3,0,2,1:T(8,128)(2,1)S(1)} %copy.56) | copy-start | bytes 1376260
  22.5 39.5 %copy-start.31 = (bf16[48,2,7,128]{3,0,2,1:T(8,128)(2,1)}, bf16[48,2,7,128]{3,0,2,1:T(8,128)(2,1)S(1)}, u32[]{:S(2)}) copy-start(bf16[48,2,7,128]{3,0,2,1:T(8,128)(2,1)S(1)} %copy.57) | copy-start | bytes 516100
  52.9 9.1 %copy-start.29 = (pred[176,1408]{1,0:T(8,128)(4,1)}, pred[176,1408]{1,0:T(8,128)(4,1)S(1)}, u32[]{:S(2)}) copy-start(pred[176,1408]{1,0:T(8,128)(4,1)S(1)} %pad_add_fusion) | copy-start | bytes 743428
  53.7 8.3 %copy-start.12 = (bf16[384,256]{1,0:T(8,128)(2,1)}, bf16[384,256]{1,0:T(8,128)(2,1)S(1)}, u32[]{:S(2)}) copy-start(bf16[384,256]{1,0:T(8,128)(2,1)S(1)} %get-tuple-element.35) | copy-start | bytes 589828
  56.7 5.3 %copy-start.4 = (bf16[1024,256]{1,0:T(8,128)(2,1)}, bf16[1024,256]{1,0:T(8,128)(2,1)S(1)}, u32[]{:S(2)}) copy-start(bf16[1024,256]{1,0:T(8,128)(2,1)S(1)} %get-tuple-element.31) | copy-start | bytes 1572868
  62.0 3.9 %copy-start.6 = (bf16[1024,256]{1,0:T(8,128)(2,1)S(1)}, bf16[1024,256]{1,0:T(8,128)(2,1)}, u32[]{:S(2)}) copy-start(bf16[1024,256]{1,0:T(8,128)(2,1)} %get-tuple-element.30) | copy-start | bytes 1572868
  62.0 3.9 %copy-start.14 = (bf16[384,256]{1,0:T(8,128)(2,1)S(1)}, bf16[384,256]{1,0:T(8,128)(2,1)}, u32[]{:S(2)}) copy-start(bf16[384,256]{1,0:T(8,128)(2,1)} %get-tuple-element.34) | copy-start | bytes 589828
  62.0 3.9 %copy-start.19 = (bf16[176,1,7,128]{3,2,1,0:T(8,128)(2,1)S(1)}, bf16[176,1,7,128]{3,2,1,0:T(8,128)(2,1)}, u32[]{:S(2)}) copy-start(bf16[176,1,7,128]{3,2,1,0:T(8,128)(2,1)} %get-tuple-element.32) | copy-start | bytes 946180
  74.2 5.6 %copy-start.7 = (bf16[1024,256]{1,0:T(8,128)(2,1)S(1)}, bf16[1024,256]{1,0:T(8,128)(2,1)}, u32[]{:S(2)}) copy-start(bf16[1024,256]{1,0:T(8,128)(2,1)} %get-tuple-element.30) | copy-start | bytes 1572868
  74.2 5.6 %copy-start.15 = (bf16[384,256]{1,0:T(8,128)(2,1)S(1)}, bf16[384,256]{1,0:T(8,128)(2,1)}, u32[]{:S(2)}) copy-start(bf16[384,256]{1,0:T(8,128)(2,1)} %get-tuple-element.34) | copy-start | bytes 589828
  74.2 5.6 %copy-start.21 = (bf16[176,1,7,128]{3,2,1,0:T(8,128)(2,1)S(1)}, bf16[176,1,7,128]{3,2,1,0:T(8,128)(2,1)}, u32[]{:S(2)}) copy-start(bf16[176,1,7,128]{3,2,1,0:T(8,128)(2,1)} %get-tuple-element.33) | copy-start | bytes 946180
  78.0 1.8 copy-start
  78.0 3.1 %copy-start.23 = (bf16[128,7,176]{0,2,1:T(8,128)(2,1)S(1)}, bf16[128,7,176]{0,2,1:T(8,128)(2,1)}, u32[]{:S(2)}) copy-start(bf16[128,7,176]{0,2,1:T(8,128)(2,1)} %get-tuple-element.47) | copy-start | bytes 946180
  89.4 24.2 %all-to-all-start.1 = ((bf16[176,16,8,14]{0,1,3,2:T(8,128)(2,1)}), bf16[176,16,8,14]{0,1,3,2:T(8,128)(2,1)}, u32[]{:S(2)}, u32[]{:S(2)}) async-start(bf16[176,16,8,14]{0,1,3,2:T(8,128)(2,1)} %copy.66), calls=%async_computation.1 | async-start | bytes 1835008 | tf_op jit(solution)/shard_map/all_to_all | solution.py:58
  94.4 2.1 copy-start.1
  94.4 2.2 copy-start.22
  96.6 9.6 %copy-start.18 = (bf16[1408,128]{0,1:T(8,128)(2,1)}, bf16[1408,128]{0,1:T(8,128)(2,1)S(1)}, u32[]{:S(2)}) copy-start(bf16[1408,128]{0,1:T(8,128)(2,1)S(1)} %convolution_bitcast_fusion) | copy-start | bytes 1081348
  96.6 1.2 copy-start.8
  96.6 1.2 copy-start.16
  96.6 6.5 %slice-start = ((s8[6938624]{0:T(1024)(128)(4,1)}), s8[4194304]{0:T(1024)(128)(4,1)S(1)}, s32[]{:S(2)}) async-start(s8[6938624]{0:T(1024)(128)(4,1)} %bitcast.155), calls=%async_computation.5 | async-start | bytes 8388608
  97.8 4.5 %copy-start.27 = (bf16[128,2,7,128]{3,0,2,1:T(8,128)(2,1)S(1)}, bf16[128,2,7,128]{3,0,2,1:T(8,128)(2,1)}, u32[]{:S(2)}) copy-start(bf16[128,2,7,128]{3,0,2,1:T(8,128)(2,1)} %copy-done.26) | copy-start | bytes 1376260
  97.8 4.5 %copy-start.32 = (bf16[48,2,7,128]{3,0,2,1:T(8,128)(2,1)S(1)}, bf16[48,2,7,128]{3,0,2,1:T(8,128)(2,1)}, u32[]{:S(2)}) copy-start(bf16[48,2,7,128]{3,0,2,1:T(8,128)(2,1)} %copy-done.31) | copy-start | bytes 516100
  97.8 5.3 %slice-start.1 = ((s8[6938624]{0:T(1024)(128)(4,1)}), s8[2744320]{0:T(1024)(128)(4,1)S(1)}, s32[]{:S(2)}) async-start(s8[6938624]{0:T(1024)(128)(4,1)} %bitcast.155), calls=%async_computation.6 | async-start | bytes 5488640
  102.4 3.0 %copy-start.9 = (bf16[7,176,1408]{2,1,0:T(8,128)(2,1)}, bf16[7,176,1408]{2,1,0:T(8,128)(2,1)S(1)}, u32[]{:S(2)}) copy-start(bf16[7,176,1408]{2,1,0:T(8,128)(2,1)S(1)} %fusion.7) | copy-start | bytes 10407940
  102.4 1.3 copy-start.20
  105.4 1.9 copy-start.11
  113.6 81.7 %all-to-all-start = ((bf16[8,176,512]{2,1,0:T(8,128)(2,1)}), bf16[8,176,512]{2,1,0:T(8,128)(2,1)S(1)}, u32[]{:S(2)}, u32[]{:S(2)}) async-start(bf16[8,176,512]{2,1,0:T(8,128)(2,1)} %pad_maximum_fusion), calls=%async_computation | async-start | bytes 2883584 | tf_op jit(solution)/shard_map/all_to_all | solution.py:21
  193.8 8.4 %copy-start.13 = (bf16[384,256]{1,0:T(8,128)(2,1)S(1)}, bf16[384,256]{1,0:T(8,128)(2,1)}, u32[]{:S(2)}) copy-start(bf16[384,256]{1,0:T(8,128)(2,1)} %copy-done.12) | copy-start | bytes 589828
  195.3 33.2 %all-to-all-start.2 = ((bf16[16,14,3584]{2,1,0:T(8,128)(2,1)}), bf16[16,14,3584]{2,1,0:T(8,128)(2,1)S(1)}, u32[]{:S(2)}, u32[]{:S(2)}) async-start(bf16[16,14,3584]{2,1,0:T(8,128)(2,1)} %reshape.99), calls=%async_computation.2 | async-start | bytes 3670016 | tf_op jit(solution)/shard_map/all_to_all | solution.py:21
  202.2 3.3 %copy-start.5 = (bf16[1024,256]{1,0:T(8,128)(2,1)S(1)}, bf16[1024,256]{1,0:T(8,128)(2,1)}, u32[]{:S(2)}) copy-start(bf16[1024,256]{1,0:T(8,128)(2,1)} %copy-done.4) | copy-start | bytes 1572868
  202.2 3.3 %copy-start.10 = (bf16[7,176,1408]{2,1,0:T(8,128)(2,1)S(1)}, bf16[7,176,1408]{2,1,0:T(8,128)(2,1)}, u32[]{:S(2)}) copy-start(bf16[7,176,1408]{2,1,0:T(8,128)(2,1)} %copy-done.9) | copy-start | bytes 10407940
  205.6 1.1 copy-start.2
  206.7 0.8 copy-start.3
  217.3 0.7 copy-start.17
Sparse Core Ops, SparseCore 0:
  10.2 41.7 all-gather.2
  53.7 133.3 all-gather.4
where the time goes:
time: 238 us; the launch traced here: 236 us
  waiting for transfers between devices  72.4 us (30%)
  matrix products  45.3 us (19%)
  local copies, waits for them, and re-layouts  36.1 us (15%)
  blocking collectives  29.9 us (13%)
  starting transfers between devices  19.1 us (8%)
  other arithmetic  19 us (8%)
  between operations  14.7 us (6%)
    all_gather x1, waiting for transfers between devices, weight_gradient(): tree_grad = lax.all_gather(upstream, 'seq', axis=0, tiled=True)  62.9 us
    all_gather x1, blocking collectives, side_by_side(): filled = lax.all_gather(both, axis, axis=dim, tiled=True)  29.9 us
    all_to_all x2, starting transfers between devices, sum_at_owner(): lax.all_to_all(cut_along(value, dim, peers), axis, 0, 0, tiled=True)  14 us
    unnamed x90, local copies, waits for them, and re-layouts  11.9 us
    sub x2, matrix products, body(): shifted = jnp.exp(scores - jnp.max(scores, axis=2, keepdims=True))  11.8 us
    dot_general x1, matrix products, body(): lax.dot_general(upstream, out_weight, (((1,), (1,)), ((), ())), preferred...  8.98 us
    convert_element_type x2, other arithmetic, body(): weights = probabilities.astype(jnp.bfloat16)  7.6 us
    dot_general x1, matrix products, weight_gradient(): lax.dot_general(picked, tree_grad, (((0,), (0,)), ((), ())), preferred_el...  6.73 us
  transfers between devices with their start and end apart: 5, of which 3 were waited for; matrix products, arithmetic and copies ran while one was open for 39% of the time, Pallas kernels for 0%

commit v1 on v0

v1 whole, which is shorter than its diff:
```python
import functools
import math

import jax
import jax.numpy as jnp
import numpy as np
from jax import lax
from jax.experimental import pallas as pl
from jax.experimental.pallas import tpu as pltpu
from jax.sharding import PartitionSpec as P

MESH = pl.DeviceIdType.MESH
HEAD = 128
HEADS = 14
GROUPS = 2
PER_KV = 7
WIDTH = HEADS * HEAD
D = 3584
PROMPT = 128
LEAF = 48
ROWS = PROMPT + LEAF
PEERS = 8
KEYS = PEERS * ROWS
TOKENS = 16 * KEYS
SHARE = 14
CHUNK = 16 * SHARE
SCALE = 1.0 / math.sqrt(HEAD)
LOG2E = 1.0 / math.log(2.0)
NEG = -1e30
PARTS = ((0, 1536), (1536, 1024), (2560, 1024))
VMEM = pltpu.MemorySpace.VMEM
LIMIT = 60 * 1024 * 1024
F32 = jnp.float32
BF16 = jnp.bfloat16


def nt(a, b):
    return lax.dot_general(a, b, (((1,), (1,)), ((), ())), preferred_element_type=F32)


def nn(a, b):
    return lax.dot_general(a, b, (((1,), (0,)), ((), ())), preferred_element_type=F32)


def tn(a, b):
    return lax.dot_general(a, b, (((0,), (0,)), ((), ())), preferred_element_type=F32)


def send_to(src, dst, send_sem, recv_sem, device):
    return pltpu.make_async_remote_copy(
        src_ref=src,
        dst_ref=dst,
        send_sem=send_sem,
        recv_sem=recv_sem,
        device_id=device,
        device_id_type=MESH,
    )


def flip(value, bit):
    low = (value // bit) % 2
    return value + bit - 2 * bit * low


def seq_peers(seq):
    found = []
    for d in range(1, PEERS):
        p = seq
        for bit in (1, 2, 4):
            if d & bit:
                p = flip(p, bit)
        found.append(p)
    return found


def gather_kernel(
    pk, pv, lk, lv, pdy, ldy, w, kv, g, yp, dy, wbuf,
    lsem, dsem, wsem, ssem, rsem, ysend, yrecv,
):
    leaf = lax.axis_index("leaf")
    seq = lax.axis_index("seq")
    twin = (flip(leaf, 1), seq)
    peers = seq_peers(seq)
    mine = [
        pltpu.make_async_copy(pk, kv.at[seq, 0:PROMPT, 0:256], lsem.at[0]),
        pltpu.make_async_copy(pv, kv.at[seq, 0:PROMPT, 256:512], lsem.at[1]),
        pltpu.make_async_copy(lk, kv.at[seq, PROMPT:ROWS, 0:256], lsem.at[2]),
        pltpu.make_async_copy(lv, kv.at[seq, PROMPT:ROWS, 256:512], lsem.at[3]),
    ]
    for c in mine:
        c.start()
    ups = [
        pltpu.make_async_copy(pdy, dy.at[0:PROMPT], dsem.at[0]),
        pltpu.make_async_copy(ldy, dy.at[PROMPT:ROWS], dsem.at[1]),
    ]
    for c in ups:
        c.start()
    tiles = WIDTH // 256
    for t in range(tiles):
        pltpu.make_async_copy(w.at[t * 256:(t + 1) * 256], wbuf.at[t], wsem.at[t]).start()
    barrier = pltpu.get_barrier_semaphore()
    for p in peers:
        pl.semaphore_signal(barrier, inc=1, device_id=(leaf, p), device_id_type=MESH)
    pl.semaphore_signal(barrier, inc=1, device_id=twin, device_id_type=MESH)
    pl.semaphore_wait(barrier, PEERS)
    for c in mine:
        c.wait()
    out = []
    for i, p in enumerate(peers):
        c = send_to(kv.at[seq], kv.at[seq], ssem.at[i], rsem.at[i], (leaf, p))
        c.start()
        out.append(c)
    ys = [
        send_to(pdy, yp.at[0:PROMPT], ysend.at[0], yrecv.at[0], twin),
        send_to(ldy, yp.at[PROMPT:ROWS], ysend.at[1], yrecv.at[1], twin),
    ]
    for c in ys:
        c.start()
    for c in ups:
        c.wait()

    def tile(t, carry):
        pltpu.make_async_copy(w.at[0:256], wbuf.at[t], wsem.at[t]).wait()
        acc = nt(dy[...], wbuf[t]).astype(BF16)
        g[2 * t] = acc[:, 0:HEAD]
        g[2 * t + 1] = acc[:, HEAD:256]
        return carry

    lax.fori_loop(0, tiles, tile, 0)
    for i, p in enumerate(peers):
        send_to(kv.at[p], kv.at[p], ssem.at[i], rsem.at[i], (leaf, p)).wait_recv()
    for c in out:
        c.wait_send()
    for c in ys:
        c.wait()


def gather_call(pk, pv, lk, lv, pdy, ldy, w):
    any_ = pl.BlockSpec(memory_space=pl.ANY)
    vm = pl.BlockSpec(memory_space=VMEM)
    return pl.pallas_call(
        gather_kernel,
        out_shape=(
            jax.ShapeDtypeStruct((PEERS, ROWS, 512), BF16),
            jax.ShapeDtypeStruct((HEADS, ROWS, HEAD), BF16),
            jax.ShapeDtypeStruct((ROWS, D), BF16),
        ),
        in_specs=[any_] * 7,
        out_specs=(vm, vm, any_),
        scratch_shapes=[
            pltpu.VMEM((ROWS, D), BF16),
            pltpu.VMEM((WIDTH // 256, 256, D), BF16),
            pltpu.SemaphoreType.DMA((4,)),
            pltpu.SemaphoreType.DMA((2,)),
            pltpu.SemaphoreType.DMA((WIDTH // 256,)),
            pltpu.SemaphoreType.DMA((PEERS - 1,)),
            pltpu.SemaphoreType.DMA((PEERS - 1,)),
            pltpu.SemaphoreType.DMA((2,)),
            pltpu.SemaphoreType.DMA((2,)),
        ],
        compiler_params=pltpu.CompilerParams(
            collective_id=0, has_side_effects=True, vmem_limit_bytes=LIMIT
        ),
        name="gather",
    )(pk, pv, lk, lv, pdy, ldy, w)


def attention_kernel(
    pq, lq, kv, g, bias, dqp, dql, atp, dkv, qs, ws, ds, at, perm
):
    for h in range(HEADS):
        cols = slice(h * HEAD, (h + 1) * HEAD)
        qs[h, 0:PROMPT, :] = pq[:, cols]
        qs[h, PROMPT:ROWS, :] = lq[:, cols]
    for grp in range(GROUPS):
        key = kv[:, grp * HEAD:(grp + 1) * HEAD]
        value = kv[:, 256 + grp * HEAD:256 + (grp + 1) * HEAD]

        def head(j, carry):
            h = grp * PER_KV + j
            q = qs[h]
            gh = g[h]
            s = nt(q, key) * (SCALE * LOG2E) + bias[...]
            top = jnp.max(s, axis=1, keepdims=True)
            e = jnp.exp2(s - top)
            total = jnp.sum(e, axis=1, keepdims=True)
            prob = e / total
            weight = prob.astype(BF16)
            ws[j] = weight
            a = nn(weight, value).astype(BF16).astype(F32)
            at[pl.ds(pl.multiple_of(h * HEAD, HEAD), HEAD), :] = a.T
            dot = jnp.sum(gh.astype(F32) * a, axis=1, keepdims=True)
            dp = nt(gh, value)
            dsc = (prob * ((dp - dot) * SCALE)).astype(BF16)
            ds[j] = dsc
            dq = nn(dsc, key)
            cols = pl.ds(pl.multiple_of(h * HEAD, HEAD), HEAD)
            dqp[:, cols] = dq[0:PROMPT]
            dql[:, cols] = dq[PROMPT:ROWS]
            return carry

        lax.fori_loop(0, PER_KV, head, 0)
        stack = slice(grp * PER_KV, (grp + 1) * PER_KV)
        tall = PER_KV * ROWS
        dk = tn(qs[stack].reshape(tall, HEAD), ds[...].reshape(tall, KEYS))
        dkv[:, grp * HEAD:(grp + 1) * HEAD] = dk.T.astype(BF16)
        dv = tn(g[stack].reshape(tall, HEAD), ws[...].reshape(tall, KEYS))
        dkv[:, 256 + grp * HEAD:256 + (grp + 1) * HEAD] = dv.T.astype(BF16)
    for c in range(2):
        for y in range(4):
            for zh in range(2):
                n = y * 448 + zh * 224 + c * 112
                atp[0, c, y, zh * 112:(zh + 1) * 112, :] = at[n:n + 112, :].astype(BF16)
        for x in range(4):
            for y in range(4):
                for z in range(4):
                    n = y * 448 + (z // 2) * 224 + c * 112 + (z % 2) * 56 + x * SHARE
                    r = x * CHUNK + y * 56 + z * SHARE
                    perm[0, r:r + SHARE, :] = at[n:n + SHARE, :]
                    r = z * CHUNK + x * 56 + y * SHARE
                    perm[1, r:r + SHARE, :] = at[n:n + SHARE, :]
        for k in range(4):
            atp[1, c, k] = perm[0, k * CHUNK:(k + 1) * CHUNK, :].astype(BF16)
            atp[2, c, k] = perm[1, k * CHUNK:(k + 1) * CHUNK, :].astype(BF16)


def attention_call(pq, lq, kv, g, bias):
    vm = pl.BlockSpec(memory_space=VMEM)
    return pl.pallas_call(
        attention_kernel,
        out_shape=(
            jax.ShapeDtypeStruct((PROMPT, WIDTH), F32),
            jax.ShapeDtypeStruct((LEAF, WIDTH), F32),
            jax.ShapeDtypeStruct((3, 2, 4, CHUNK, ROWS), BF16),
            jax.ShapeDtypeStruct((KEYS, 512), BF16),
        ),
        in_specs=[vm] * 5,
        out_specs=(vm,) * 4,
        scratch_shapes=[
            pltpu.VMEM((HEADS, ROWS, HEAD), BF16),
            pltpu.VMEM((PER_KV, ROWS, KEYS), BF16),
            pltpu.VMEM((PER_KV, ROWS, KEYS), BF16),
            pltpu.VMEM((WIDTH, ROWS), F32),
            pltpu.VMEM((2, 4 * CHUNK, ROWS), F32),
        ],
        compiler_params=pltpu.CompilerParams(vmem_limit_bytes=LIMIT),
        name="attention",
    )(pq, lq, kv, g, bias)


def reduce_kernel(
    atp, pdy, ldy, yp, dkv, wg, dk, dv, *scratch
):
    (yo, yt, ap) = scratch[0:3]
    pb = scratch[3:6]
    own = scratch[6:9]
    rel = scratch[9:12]
    rin = scratch[12:15]
    b2 = scratch[15:18]
    r2 = scratch[18:21]
    b3 = scratch[21:24]
    r3 = scratch[24:27]
    (kin, lsem, asend, arecv, ksend, krecv, s1, v1, s2, v2, s3, v3) = scratch[27:]
    leaf = lax.axis_index("leaf")
    seq = lax.axis_index("seq")
    core = leaf % 2
    y = leaf // 4
    z = ((leaf // 2) % 2) * 2 + seq // 4
    x = seq % 4
    twin = (flip(leaf, 1), seq)
    peers = seq_peers(seq)

    def on_x(k):
        return (leaf, (seq // 4) * 4 + (x + k) % 4)

    def on_y(k):
        return (((y + k) % 4) * 4 + leaf % 4, seq)

    def on_z(k):
        other = (z + k) % 4
        return (y * 4 + (other // 2) * 2 + core, (other % 2) * 4 + x)

    axes = ((on_y, on_z, on_x), (on_x, on_y, on_z), (on_z, on_x, on_y))
    spots = ((y, z, x), (x, y, z), (z, x, y))

    loads = [
        pltpu.make_async_copy(pdy, yo.at[0:PROMPT], lsem.at[0]),
        pltpu.make_async_copy(ldy, yo.at[PROMPT:ROWS], lsem.at[1]),
        pltpu.make_async_copy(yp, yt, lsem.at[2]),
    ]
    for c in loads:
        c.start()
    barrier = pltpu.get_barrier_semaphore()
    greet = [(leaf, p) for p in peers] + [twin]
    greet += [on_y(k) for k in (1, 2, 3)] + [on_z(k) for k in (1, 2, 3)]
    for d in greet:
        pl.semaphore_signal(barrier, inc=1, device_id=d, device_id_type=MESH)
    pl.semaphore_wait(barrier, len(greet))

    swaps = []
    for p in range(3):
        c = send_to(atp.at[p, 1 - core], ap.at[p], asend.at[p], arecv.at[p], twin)
        c.start()
        swaps.append(c)
    for c in loads:
        c.wait()
    for c in swaps:
        c.wait_recv()

    started = []

    def go(src, dst, send_sem, recv_sem, device):
        c = send_to(src, dst, send_sem, recv_sem, device)
        c.start()
        started.append(c)
        return c

    def product(p, k):
        first, wide = PARTS[p]
        dest = (spots[p][0] + k) % 4
        cols = slice(first, first + wide)
        return nn(atp[p, core, dest], yo[:, cols]) + nn(ap[p, dest], yt[:, cols])

    relays = {}
    direct = {}
    for p in range(3):
        h = PARTS[p][1] // 2
        pb[p][2] = product(p, 2).astype(BF16)
        relays[p, 0] = go(pb[p].at[2, :, 0:h], rel[p].at[0], s1.at[p, 0], v1.at[p, 0], axes[p][0](1))
        relays[p, 1] = go(pb[p].at[2, :, h:2 * h], rel[p].at[1], s1.at[p, 1], v1.at[p, 1], axes[p][0](3))
    for p in range(3):
        h = PARTS[p][1] // 2
        pb[p][1] = product(p, 1).astype(BF16)
        direct[p, 0] = go(pb[p].at[1, :, h:2 * h], rin[p].at[0, :, h:2 * h], s1.at[p, 2], v1.at[p, 2], axes[p][0](1))
        pb[p][3] = product(p, 3).astype(BF16)
        direct[p, 1] = go(pb[p].at[3, :, 0:h], rin[p].at[1, :, 0:h], s1.at[p, 3], v1.at[p, 3], axes[p][0](3))
    for p in range(3):
        own[p][...] = product(p, 0)
    for p in (1, 2, 0):
        h = PARTS[p][1] // 2
        relays[p, 0].wait_recv()
        pb[p][1, :, 0:h] = (pb[p][1, :, 0:h].astype(F32) + rel[p][0].astype(F32)).astype(BF16)
        direct[p, 2] = go(pb[p].at[1, :, 0:h], rin[p].at[0, :, 0:h], s1.at[p, 4], v1.at[p, 4], axes[p][0](1))
        relays[p, 1].wait_recv()
        pb[p][3, :, h:2 * h] = (pb[p][3, :, h:2 * h].astype(F32) + rel[p][1].astype(F32)).astype(BF16)
        direct[p, 3] = go(pb[p].at[3, :, h:2 * h], rin[p].at[1, :, h:2 * h], s1.at[p, 5], v1.at[p, 5], axes[p][0](3))
    grads = []
    for i, q in enumerate(peers):
        grads.append(go(dkv.at[q], kin.at[i], ksend.at[i], krecv.at[i], (leaf, q)))
    second = {}
    for p in (1, 2, 0):
        wide = PARTS[p][1]
        for i in range(4):
            direct[p, i].wait_recv()
        pad = jnp.zeros((8, wide), F32)
        for j in range(4):
            rows = slice(j * 56, (j + 1) * 56)
            full = own[p][rows] + rin[p][0, rows].astype(F32) + rin[p][1, rows].astype(F32)
            b2[p][j] = jnp.concatenate([full, pad], axis=0).astype(BF16)
        spot = spots[p][1]
        for k in (2, 1, 3):
            second[p, k] = go(b2[p].at[(spot + k) % 4], r2[p].at[k - 1], s2.at[p, k - 1], v2.at[p, k - 1], axes[p][1](k))
    third = {}
    for p in (1, 2, 0):
        for k in (1, 2, 3):
            second[p, k].wait_recv()
        full = b2[p][spots[p][1]].astype(F32)
        for k in range(3):
            full = full + r2[p][k].astype(F32)
        pad = jnp.zeros((2, PARTS[p][1]), F32)
        for j in range(4):
            piece = full[j * SHARE:(j + 1) * SHARE]
            b3[p][j] = jnp.concatenate([piece, pad], axis=0).astype(BF16)
        spot = spots[p][2]
        for k in (2, 1, 3):
            third[p, k] = go(b3[p].at[(spot + k) % 4], r3[p].at[k - 1], s3.at[p, k - 1], v3.at[p, k - 1], axes[p][2](k))
    for c in grads:
        c.wait_recv()
    block = dkv[seq].astype(F32)
    for i in range(PEERS - 1):
        block = block + kin[i].astype(F32)
    dk[...] = block[:, 0:256]
    dv[...] = block[:, 256:512]
    for p in (1, 2, 0):
        first, wide = PARTS[p]
        for k in (1, 2, 3):
            third[p, k].wait_recv()
        full = b3[p][spots[p][2]].astype(F32)
        for k in range(3):
            full = full + r3[p][k].astype(F32)
        wg[:, first:first + wide] = full[0:SHARE] * (1.0 / math.sqrt(TOKENS))
    for c in swaps:
        c.wait_send()
    for c in started:
        c.wait_send()


def reduce_call(atp, pdy, ldy, yp, dkv):
    any_ = pl.BlockSpec(memory_space=pl.ANY)
    vm = pl.BlockSpec(memory_space=VMEM)
    widths = [w for _, w in PARTS]
    dma = pltpu.SemaphoreType.DMA
    scratch = [
        pltpu.VMEM((ROWS, D), BF16),
        pltpu.VMEM((ROWS, D), BF16),
        pltpu.VMEM((3, 4, CHUNK, ROWS), BF16),
    ]
    scratch += [pltpu.VMEM((4, CHUNK, w), BF16) for w in widths]
    scratch += [pltpu.VMEM((CHUNK, w), F32) for w in widths]
    scratch += [pltpu.VMEM((2, CHUNK, w // 2), BF16) for w in widths]
    scratch += [pltpu.VMEM((2, CHUNK, w), BF16) for w in widths]
    scratch += [pltpu.VMEM((4, 64, w), BF16) for w in widths]
    scratch += [pltpu.VMEM((3, 64, w), BF16) for w in widths]
    scratch += [pltpu.VMEM((4, 16, w), BF16) for w in widths]
    scratch += [pltpu.VMEM((3, 16, w), BF16) for w in widths]
    scratch += [pltpu.VMEM((PEERS - 1, ROWS, 512), BF16), dma((3,)), dma((3,)), dma((3,))]
    scratch += [dma((PEERS - 1,)), dma((PEERS - 1,)), dma((3, 6)), dma((3, 6))]
    scratch += [dma((3, 3)), dma((3, 3)), dma((3, 3)), dma((3, 3))]
    return pl.pallas_call(
        reduce_kernel,
        out_shape=(
            jax.ShapeDtypeStruct((SHARE, D), F32),
            jax.ShapeDtypeStruct((ROWS, 256), F32),
            jax.ShapeDtypeStruct((ROWS, 256), F32),
        ),
        in_specs=[vm, any_, any_, any_, vm],
        out_specs=(vm, vm, vm),
        scratch_shapes=scratch,
        compiler_params=pltpu.CompilerParams(
            collective_id=1, has_side_effects=True, vmem_limit_bytes=LIMIT
        ),
        name="reduce",
    )(atp, pdy, ldy, yp, dkv)


def visibility_bias(lengths, offsets, parents):
    seq = lax.axis_index("seq")
    slot, row = np.divmod(np.arange(KEYS), ROWS)
    key_is_prompt = jnp.asarray(row < PROMPT)
    key_index = jnp.asarray(np.where(row < PROMPT, slot * PROMPT + row, slot * LEAF + row - PROMPT), jnp.int32)
    ends = jnp.cumsum(lengths)
    ids = jnp.arange(lengths.shape[0], dtype=jnp.int32)
    query_leaf = seq * LEAF + jnp.arange(LEAF, dtype=jnp.int32)
    query_prompt = seq * PROMPT + jnp.arange(PROMPT, dtype=jnp.int32)
    key_branch = jnp.sum((key_index[:, None] >= ends[None, :]).astype(jnp.int32), axis=1)
    query_branch = jnp.sum((query_leaf[:, None] >= ends[None, :]).astype(jnp.int32), axis=1)
    member = (query_branch[:, None] == ids[None, :]).astype(jnp.int32)
    fork = jnp.sum(member * offsets[None, :], axis=1)
    ancestor = jnp.sum(member * parents[None, :], axis=1)
    prompt_sees = key_is_prompt[None, :] & (key_index[None, :] <= query_prompt[:, None])
    same = (key_branch[None, :] == query_branch[:, None]) & (key_index[None, :] <= query_leaf[:, None])
    inherited = (key_branch[None, :] == ancestor[:, None]) & (ancestor[:, None] != query_branch[:, None])
    leaf_sees = jnp.where(key_is_prompt[None, :], key_index[None, :] < fork[:, None], same | inherited)
    sees = jnp.concatenate([prompt_sees, leaf_sees], axis=0)
    return jnp.where(sees, 0.0, NEG).astype(F32)


def body(pq, pk, pv, lq, lk, lv, pdy, ldy, w, lengths, offsets, parents):
    bias = visibility_bias(lengths[0], offsets[0], parents[0])
    kv, g, yp = gather_call(pk[0], pv[0], lk[0], lv[0], pdy[0], ldy[0], w)
    dqp, dql, atp, dkv = attention_call(pq[0], lq[0], kv.reshape(KEYS, 512), g, bias)
    wg, dk, dv = reduce_call(atp, pdy[0], ldy[0], yp, dkv.reshape(PEERS, ROWS, 512))
    return (
        dqp[None], dk[None, :PROMPT], dv[None, :PROMPT],
        dql[None], dk[None, PROMPT:], dv[None, PROMPT:], wg,
    )


def solution(mesh):
    rows = P("leaf", "seq", None)
    placed = (rows,) * 8 + (P(),) + (P("leaf", None),) * 3
    return jax.shard_map(
        body,
        mesh=mesh,
        in_specs=placed,
        out_specs=(rows,) * 6 + (P(("leaf", "seq"), None),),
        check_vma=False,
    )
```

time: 238 us -> 122 us (0.51)
  Pallas kernels: 0 us -> 110 us
  waiting for transfers between devices: 72.4 us -> 0 us
  matrix products: 45.3 us -> 0 us
  local copies, waits for them, and re-layouts: 36.1 us -> 5.52 us
  blocking collectives: 29.9 us -> 0 us
  starting transfers between devices: 19.1 us -> 0 us
  other arithmetic: 19 us -> 4.63 us
  between operations: 14.7 us -> 0.69 us
    pallas_call x0 -> x3, Pallas kernels: none -> 110 us  [the longest x1 58.2 us: reduce_call(): pl.pallas_call(reduce_kernel, out_shape=(jax.ShapeDtypeStruct((SHARE, D),...]
    all_gather x2 -> x0, waiting for transfers between devices: 62.9 us -> none  [the longest x1 62.9 us: weight_gradient(): tree_grad = lax.all_gather(upstream, 'seq', axis=0, tiled=True)]
    dot_general x12 -> x0, matrix products: 33.4 us -> none  [the longest x1 8.98 us: body(): lax.dot_general(upstream, out_weight, (((1,), (1,)), ((), ())), preferred...]
    all_gather x1 -> x0, blocking collectives: 29.9 us -> none  [side_by_side(): filled = lax.all_gather(both, axis, axis=dim, tiled=True)]
    all_to_all x3 -> x0, starting transfers between devices: 19 us -> none  [the longest x2 14 us: sum_at_owner(): lax.all_to_all(cut_along(value, dim, peers), axis, 0, 0, tiled=True)]
    sub x2 -> x0, matrix products: 11.8 us -> none  [body(): shifted = jnp.exp(scores - jnp.max(scores, axis=2, keepdims=True))]
    unnamed x90 -> x1, local copies, waits for them, and re-layouts: 11.9 us -> 1.64 us
    all_to_all x3 -> x0, waiting for transfers between devices: 9.5 us -> none  [the longest x2 6.43 us: sum_at_owner(): lax.all_to_all(cut_along(value, dim, peers), axis, 0, 0, tiled=True)]
  transfers between devices with their start and end apart: 5 -> 0, of which waited for: 3 -> 0; matrix products, arithmetic and copies ran while one was open for 39% -> 0% of each run, Pallas kernels for 0% -> 0%
where the time goes in v1:
time: 122 us; the launch traced here: 121 us
  Pallas kernels  110 us (90%)
  local copies, waits for them, and re-layouts  5.52 us (5%)
  other arithmetic  4.63 us (4%)
    pallas_call x1, Pallas kernels, reduce_call(): pl.pallas_call(reduce_kernel, out_shape=(jax.ShapeDtypeStruct((SHARE, D),...  58.2 us
    pallas_call x1, Pallas kernels, gather_call(): pl.pallas_call(gather_kernel, out_shape=(jax.ShapeDtypeStruct((PEERS, ROW...  28.3 us
    pallas_call x1, Pallas kernels, attention_call(): pl.pallas_call(attention_kernel, out_shape=(jax.ShapeDtypeStruct((PROMPT,...  23.7 us

profile of v1, /device:TPU:0, one launch (start us, length us, event | category | flops | bytes accessed | tf_op | source)
XLA Modules:
  0.0 121.1 jit_solution(1626513867591896350)
XLA Ops:
  0.7 0.7 copy.23
  1.4 0.1 reduce.1
  1.6 0.1 convert_reduce_fusion.1
  1.6 0.8 select_reduce_fusion.1
  2.4 0.8 convert_reduce_fusion
  3.2 0.9 or_select_fusion
  4.1 0.9 compare_and_fusion
  5.0 1.0 add_select_fusion.bias
  6.0 28.3 %gather.1 = (bf16[8,176,512]{2,1,0:T(8,128)(2,1)}, bf16[14,176,128]{2,1,0:T(8,128)(2,1)}, bf16[176,3584]{1,0:T(8,128)(2,1)}) custom-call(bf16[128,256]{1,0:T(8,128)(2,1)} %bitcast.31, bf16[128,256]{1,0:T(8,128)(2,1)} %bitcast.32, bf16[48,256]{1,0:T(8,128)(2,1)} %bitcast.33, bf16[48,256]{1,0:T(8,128)(2,1)} %bitcast.34, bf16[128,3584]{1,0:T(8,128)(2,1)} %bitcast.23, ...), custom_call_target="tpu_custom_call" | custom-call | tf_op jit(solution)/shard_map/gather/pallas_call | solution.py:141
  34.4 23.7 %attention.1 = (f32[128,1792]{1,0:T(8,128)}, f32[48,1792]{1,0:T(8,128)}, bf16[3,2,4,224,176]{4,3,2,1,0:T(8,128)(2,1)}, bf16[1408,512]{1,0:T(8,128)(2,1)}) custom-call(bf16[128,1792]{1,0:T(8,128)(2,1)} %bitcast.29, bf16[48,1792]{1,0:T(8,128)(2,1)} %bitcast.30, bf16[1408,512]{1,0:T(8,128)(2,1)} %bitcast.25, bf16[14,176,128]{2,1,0:T(8,128)(2,1)} %get-tuple-element.18.g, ...), custom_call_target="tpu_custom_call" | custom-call | tf_op jit(solution)/shard_map/attention/pallas_call | solution.py:229
  58.1 58.2 %reduce.2 = (f32[14,3584]{1,0:T(8,128)}, f32[176,256]{1,0:T(8,128)}, f32[176,256]{1,0:T(8,128)}) custom-call(bf16[3,2,4,224,176]{4,3,2,1,0:T(8,128)(2,1)} %get-tuple-element.20.atp, bf16[128,3584]{1,0:T(8,128)(2,1)} %bitcast.24, bf16[48,3584]{1,0:T(8,128)(2,1)} %bitcast.28, bf16[176,3584]{1,0:T(8,128)(2,1)} %get-tuple-element.21.yp, ...), custom_call_target="tpu_custom_call" | custom-call | tf_op jit(solution)/shard_map/reduce/pallas_call | solution.py:419
  116.3 1.5 %slice_bitcast_fusion.2 = (f32[1,48,256]{2,1,0:T(8,128)}, f32[1,48,256]{2,1,0:T(8,128)}) fusion(f32[176,256]{1,0:T(8,128)} %get-tuple-element.24, f32[176,256]{1,0:T(8,128)} %get-tuple-element.23), kind=kLoop, calls=%fused_computation.6 | loop fusion | bytes 196608 | tf_op jit(solution)/shard_map/broadcast_in_dim | solution.py:465
  117.8 1.7 %slice_bitcast_fusion = (f32[1,128,256]{2,1,0:T(8,128)}, f32[1,128,256]{2,1,0:T(8,128)}) fusion(f32[176,256]{1,0:T(8,128)} %get-tuple-element.24, f32[176,256]{1,0:T(8,128)} %get-tuple-element.23), kind=kLoop, calls=%fused_computation.3 | loop fusion | bytes 524288 | tf_op jit(solution)/shard_map/broadcast_in_dim | solution.py:464
  119.5 1.6 %copy.25 = f32[14,3584]{1,0:T(8,128)} copy(f32[14,3584]{1,0:T(8,128)} %get-tuple-element.46) | data formatting | bytes 401408
  (4 shorter events, 0.1 us)

commit v2 on v1

v2 whole, which is shorter than its diff:
```python
import math

import jax
import jax.numpy as jnp
from jax import lax
from jax.experimental import pallas as pl
from jax.experimental.pallas import tpu as pltpu
from jax.sharding import PartitionSpec as P

MESH = pl.DeviceIdType.MESH
HEAD = 128
HEADS = 14
GROUPS = 2
PER_KV = 7
WIDTH = HEADS * HEAD
D = 3584
PROMPT = 128
LEAF = 48
ROWS = PROMPT + LEAF
PEERS = 8
KEYS = PEERS * ROWS
TOKENS = 16 * KEYS
SHARE = 14
BRANCHES = 16
CHUNK = 16 * SHARE
SCALE = 1.0 / math.sqrt(HEAD)
LOG2E = 1.0 / math.log(2.0)
NEG = -1e30
PARTS = ((0, 1536), (1536, 1024), (2560, 1024))
VMEM = pltpu.MemorySpace.VMEM
SMEM = pltpu.MemorySpace.SMEM
HALF = 256
LIMIT = 63 * 1024 * 1024
F32 = jnp.float32
BF16 = jnp.bfloat16


def nt(a, b):
    return lax.dot_general(a, b, (((1,), (1,)), ((), ())), preferred_element_type=F32)


def nn(a, b):
    return lax.dot_general(a, b, (((1,), (0,)), ((), ())), preferred_element_type=F32)


def tn(a, b):
    return lax.dot_general(a, b, (((0,), (0,)), ((), ())), preferred_element_type=F32)


def send_to(src, dst, send_sem, recv_sem, device):
    return pltpu.make_async_remote_copy(
        src_ref=src,
        dst_ref=dst,
        send_sem=send_sem,
        recv_sem=recv_sem,
        device_id=device,
        device_id_type=MESH,
    )


def flip(value, bit):
    low = (value // bit) % 2
    return value + bit - 2 * bit * low


def seq_peers(seq):
    found = []
    for d in range(1, PEERS):
        p = seq
        for bit in (1, 2, 4):
            if d & bit:
                p = flip(p, bit)
        found.append(p)
    return found


def visibility(lengths, offsets, parents, seq, bias):
    rows = lax.broadcasted_iota(jnp.int32, (ROWS, 1), 0)
    is_leaf = rows >= PROMPT
    query = jnp.where(is_leaf, seq * LEAF + rows - PROMPT, seq * PROMPT + rows)
    cols = lax.broadcasted_iota(jnp.int32, (1, KEYS), 1)
    slot = jnp.zeros((1, KEYS), jnp.int32)
    for s in range(1, PEERS):
        slot = slot + (cols >= s * ROWS).astype(jnp.int32)
    spot = cols - slot * ROWS
    key_leaf = spot >= PROMPT
    key = jnp.where(key_leaf, slot * LEAF + spot - PROMPT, slot * PROMPT + spot)
    key_branch = jnp.zeros((1, KEYS), jnp.int32)
    query_branch = jnp.zeros((ROWS, 1), jnp.int32)
    end = jnp.int32(0)
    for b in range(BRANCHES):
        end = end + lengths[0, b]
        key_branch = key_branch + (key >= end).astype(jnp.int32)
        query_branch = query_branch + (query >= end).astype(jnp.int32)
    fork = jnp.zeros((ROWS, 1), jnp.int32)
    ancestor = jnp.zeros((ROWS, 1), jnp.int32)
    for b in range(BRANCHES):
        here = query_branch == b
        fork = jnp.where(here, offsets[0, b], fork)
        ancestor = jnp.where(here, parents[0, b], ancestor)
    ancestor = jnp.where(is_leaf & (ancestor != query_branch), ancestor, -1)
    branch = jnp.where(is_leaf, query_branch, -1)
    reach = jnp.where(is_leaf, fork, query + 1)
    prompt_key = jnp.where(key_leaf, 1 << 20, key)
    key_branch = jnp.where(key_leaf, key_branch, -2)
    sees = prompt_key < reach
    sees = sees | ((key_branch == branch) & (key <= query))
    sees = sees | (key_branch == ancestor)
    bias[...] = jnp.where(sees, 0.0, NEG)


def tree_kernel(
    pq, pk, pv, lq, lk, lv, pdy, ldy, w, lengths, offsets, parents,
    dqp, dql, wg, dkv_out, *scratch
):
    (kv, yo, yt, wbuf, g, qs, attn, ws, ds, at, perm, atp, ap, bias, dkv, kin) = scratch[0:16]
    own = scratch[16:19]
    rel = scratch[19:22]
    rin = scratch[22:25]
    b2 = scratch[25:28]
    r2 = scratch[28:31]
    b3 = scratch[31:34]
    r3 = scratch[34:37]
    (lsem, dsem, wsem, qsem, gsend, grecv, ysend, yrecv, asend, arecv,
     ksend, krecv, s1, v1, s2, v2, s3, v3) = scratch[37:]
    leaf = lax.axis_index("leaf")
    seq = lax.axis_index("seq")
    core = leaf % 2
    y = leaf // 4
    plane = seq // 4
    z = ((leaf // 2) % 2) * 2 + plane
    x = seq % 4
    twin = (flip(leaf, 1), seq)
    peers = seq_peers(seq)

    def slot(q, k):
        return q * 4 + (x + k) % 4

    def on_x(k):
        return (leaf, slot(plane, k))

    def on_y(k):
        return (((y + k) % 4) * 4 + leaf % 4, seq)

    def on_z(k):
        other = (z + k) % 4
        return (y * 4 + (other // 2) * 2 + core, (other % 2) * 4 + x)

    across = (leaf, slot(1 - plane, 0))
    axes = ((on_y, on_z, on_x), (on_x, on_y, on_z), (on_z, on_x, on_y))
    spots = ((y, z, x), (x, y, z), (z, x, y))

    mine = [
        pltpu.make_async_copy(pk, kv.at[seq, 0:PROMPT, 0:256], lsem.at[0]),
        pltpu.make_async_copy(pv, kv.at[seq, 0:PROMPT, 256:512], lsem.at[1]),
        pltpu.make_async_copy(lk, kv.at[seq, PROMPT:ROWS, 0:256], lsem.at[2]),
        pltpu.make_async_copy(lv, kv.at[seq, PROMPT:ROWS, 256:512], lsem.at[3]),
    ]
    for c in mine:
        c.start()
    ups = [
        pltpu.make_async_copy(pdy, yo.at[0:PROMPT], dsem.at[0]),
        pltpu.make_async_copy(ldy, yo.at[PROMPT:ROWS], dsem.at[1]),
    ]
    for c in ups:
        c.start()
    tiles = WIDTH // 256
    for t in range(tiles):
        pltpu.make_async_copy(w.at[t * 256:(t + 1) * 256], wbuf.at[t], wsem.at[t]).start()
    queries = []
    for h in range(HEADS):
        cols = slice(h * HEAD, (h + 1) * HEAD)
        queries.append(pltpu.make_async_copy(pq.at[:, cols], qs.at[h, 0:PROMPT], qsem.at[h, 0]))
        queries.append(pltpu.make_async_copy(lq.at[:, cols], qs.at[h, PROMPT:ROWS], qsem.at[h, 1]))
    for c in queries:
        c.start()
    barrier = pltpu.get_barrier_semaphore()
    greet = [(leaf, p) for p in peers] + [twin]
    greet += [on_y(k) for k in (1, 2, 3)] + [on_z(k) for k in (1, 2, 3)]
    for d in greet:
        pl.semaphore_signal(barrier, inc=1, device_id=d, device_id_type=MESH)
    pl.semaphore_wait(barrier, len(greet))
    started = []

    def go(src, dst, send_sem, recv_sem, device):
        c = send_to(src, dst, send_sem, recv_sem, device)
        c.start()
        started.append(c)
        return c

    def pass_on(ref, i, device):
        return go(ref, ref, gsend.at[i], grecv.at[i], device)

    def arrived(ref, i):
        send_to(ref, ref, gsend.at[i], grecv.at[i], across).wait_recv()

    for c in mine:
        c.wait()
    block = kv.at[seq]
    pass_on(block, 0, across)
    pass_on(block, 1, on_x(1))
    pass_on(block, 2, on_x(3))
    swaps = [
        go(pdy, yt.at[0:PROMPT], ysend.at[0], yrecv.at[0], twin),
        go(ldy, yt.at[PROMPT:ROWS], ysend.at[1], yrecv.at[1], twin),
    ]
    for c in ups:
        c.wait()

    def tile(t, carry):
        pltpu.make_async_copy(w.at[0:256], wbuf.at[t], wsem.at[t]).wait()
        acc = nt(yo[...], wbuf[t]).astype(BF16)
        g[2 * t] = acc[:, 0:HEAD]
        g[2 * t + 1] = acc[:, HEAD:256]
        return carry

    lax.fori_loop(0, tiles, tile, 0)
    arrived(kv.at[slot(plane, 3)], 1)
    pass_on(kv.at[slot(plane, 3), :, 0:HALF], 3, on_x(1))
    arrived(kv.at[slot(plane, 1)], 2)
    pass_on(kv.at[slot(plane, 1), :, HALF:512], 4, on_x(3))
    arrived(kv.at[slot(1 - plane, 0)], 0)
    pass_on(kv.at[slot(1 - plane, 0)], 5, on_x(1))
    pass_on(kv.at[slot(1 - plane, 0)], 6, on_x(3))
    visibility(lengths, offsets, parents, seq, bias)
    arrived(kv.at[slot(plane, 2), :, 0:HALF], 3)
    arrived(kv.at[slot(plane, 2), :, HALF:512], 4)
    pass_on(kv.at[slot(plane, 2)], 7, across)
    for c in queries:
        c.wait()
    arrived(kv.at[slot(1 - plane, 3)], 5)
    arrived(kv.at[slot(1 - plane, 1)], 6)
    arrived(kv.at[slot(1 - plane, 2)], 7)

    def keys_of(grp):
        cols = pl.ds(pl.multiple_of(grp * HEAD, HEAD), HEAD)
        return kv[:, :, cols].reshape(KEYS, HEAD)

    def values_of(grp):
        cols = pl.ds(pl.multiple_of(256 + grp * HEAD, HEAD), HEAD)
        return kv[:, :, cols].reshape(KEYS, HEAD)

    def forward(h, carry):
        grp = h // PER_KV
        s = nt(qs[h], keys_of(grp)) * (SCALE * LOG2E) + bias[...]
        top = jnp.max(s, axis=1, keepdims=True)
        e = jnp.exp2(s - top)
        total = jnp.sum(e, axis=1, keepdims=True)
        weight = (e / total).astype(BF16)
        ws[h] = weight
        a = nn(weight, values_of(grp)).astype(BF16)
        attn[h] = a
        at[pl.ds(pl.multiple_of(h * HEAD, HEAD), HEAD), :] = a.astype(F32).T
        return carry

    lax.fori_loop(0, HEADS, forward, 0)
    for c in range(2):
        for yy in range(4):
            for zh in range(2):
                n = yy * 448 + zh * 224 + c * 112
                atp[0, c, yy, zh * 112:(zh + 1) * 112, :] = at[n:n + 112, :].astype(BF16)
        for xx in range(4):
            for yy in range(4):
                for zz in range(4):
                    n = yy * 448 + (zz // 2) * 224 + c * 112 + (zz % 2) * 56 + xx * SHARE
                    r = xx * CHUNK + yy * 56 + zz * SHARE
                    perm[0, r:r + SHARE, :] = at[n:n + SHARE, :]
                    r = zz * CHUNK + xx * 56 + yy * SHARE
                    perm[1, r:r + SHARE, :] = at[n:n + SHARE, :]
        for k in range(4):
            atp[1, c, k] = perm[0, k * CHUNK:(k + 1) * CHUNK, :].astype(BF16)
            atp[2, c, k] = perm[1, k * CHUNK:(k + 1) * CHUNK, :].astype(BF16)
    rows = []
    for p in range(3):
        rows.append(go(atp.at[p, 1 - core], ap.at[p], asend.at[p], arecv.at[p], twin))
    for c in swaps:
        c.wait_recv()
    for c in rows:
        c.wait_recv()

    def part(p, k, lo, hi):
        first = PARTS[p][0]
        return wbuf.at[k, 0:CHUNK, first + lo:first + hi]

    def product(p, k):
        first, wide = PARTS[p]
        dest = (spots[p][0] + k) % 4
        cols = slice(first, first + wide)
        return nn(atp[p, core, dest], yo[:, cols]) + nn(ap[p, dest], yt[:, cols])

    relays = {}
    direct = {}
    for p in range(3):
        wide = PARTS[p][1]
        h = wide // 2
        part(p, 2, 0, wide)[...] = product(p, 2).astype(BF16)
        relays[p, 0] = go(part(p, 2, 0, h), rel[p].at[0], s1.at[p, 0], v1.at[p, 0], axes[p][0](1))
        relays[p, 1] = go(part(p, 2, h, wide), rel[p].at[1], s1.at[p, 1], v1.at[p, 1], axes[p][0](3))
    for p in range(3):
        wide = PARTS[p][1]
        h = wide // 2
        part(p, 1, 0, wide)[...] = product(p, 1).astype(BF16)
        direct[p, 0] = go(part(p, 1, h, wide), rin[p].at[0, :, h:wide], s1.at[p, 2], v1.at[p, 2], axes[p][0](1))
        part(p, 3, 0, wide)[...] = product(p, 3).astype(BF16)
        direct[p, 1] = go(part(p, 3, 0, h), rin[p].at[1, :, 0:h], s1.at[p, 3], v1.at[p, 3], axes[p][0](3))
    for p in range(3):
        own[p][...] = product(p, 0)

    def relay(p):
        wide = PARTS[p][1]
        h = wide // 2
        relays[p, 0].wait_recv()
        here = part(p, 1, 0, h)
        here[...] = (here[...].astype(F32) + rel[p][0].astype(F32)).astype(BF16)
        direct[p, 2] = go(here, rin[p].at[0, :, 0:h], s1.at[p, 4], v1.at[p, 4], axes[p][0](1))
        relays[p, 1].wait_recv()
        here = part(p, 3, h, wide)
        here[...] = (here[...].astype(F32) + rel[p][1].astype(F32)).astype(BF16)
        direct[p, 3] = go(here, rin[p].at[1, :, h:wide], s1.at[p, 5], v1.at[p, 5], axes[p][0](3))

    grads = []
    for grp in range(GROUPS):

        def backward(j, carry):
            h = grp * PER_KV + j
            gh = g[h]
            dot = jnp.sum(gh.astype(F32) * attn[h].astype(F32), axis=1, keepdims=True)
            dp = nt(gh, values_of(grp))
            dsc = (ws[h].astype(F32) * ((dp - dot) * SCALE)).astype(BF16)
            ds[j] = dsc
            dq = nn(dsc, keys_of(grp))
            cols = pl.ds(pl.multiple_of(h * HEAD, HEAD), HEAD)
            dqp[:, cols] = dq[0:PROMPT]
            dql[:, cols] = dq[PROMPT:ROWS]
            return carry

        lax.fori_loop(0, PER_KV, backward, 0)
        stack = slice(grp * PER_KV, (grp + 1) * PER_KV)
        tall = PER_KV * ROWS
        dk = tn(qs[stack].reshape(tall, HEAD), ds[...].reshape(tall, KEYS))
        dkv[grp, :, :, 0:HEAD] = dk.T.astype(BF16).reshape(PEERS, ROWS, HEAD)
        dv = tn(g[stack].reshape(tall, HEAD), ws[stack].reshape(tall, KEYS))
        dkv[grp, :, :, HEAD:256] = dv.T.astype(BF16).reshape(PEERS, ROWS, HEAD)
        if grp == 0:
            for p in (1, 2, 0):
                relay(p)
        for i, q in enumerate(peers):
            grads.append(go(dkv.at[grp, q], kin.at[grp, i], ksend.at[grp, i], krecv.at[grp, i], (leaf, q)))
    second = {}
    for p in (1, 2, 0):
        wide = PARTS[p][1]
        for i in range(4):
            direct[p, i].wait_recv()
        pad = jnp.zeros((8, wide), F32)
        for j in range(4):
            piece = slice(j * 56, (j + 1) * 56)
            full = own[p][piece] + rin[p][0, piece].astype(F32) + rin[p][1, piece].astype(F32)
            b2[p][j] = jnp.concatenate([full, pad], axis=0).astype(BF16)
        spot = spots[p][1]
        for k in (2, 1, 3):
            second[p, k] = go(b2[p].at[(spot + k) % 4], r2[p].at[k - 1], s2.at[p, k - 1], v2.at[p, k - 1], axes[p][1](k))
    third = {}
    for p in (1, 2, 0):
        for k in (1, 2, 3):
            second[p, k].wait_recv()
        full = b2[p][spots[p][1]].astype(F32)
        for k in range(3):
            full = full + r2[p][k].astype(F32)
        pad = jnp.zeros((2, PARTS[p][1]), F32)
        for j in range(4):
            piece = full[j * SHARE:(j + 1) * SHARE]
            b3[p][j] = jnp.concatenate([piece, pad], axis=0).astype(BF16)
        spot = spots[p][2]
        for k in (2, 1, 3):
            third[p, k] = go(b3[p].at[(spot + k) % 4], r3[p].at[k - 1], s3.at[p, k - 1], v3.at[p, k - 1], axes[p][2](k))
    for c in grads:
        c.wait_recv()
    for grp in range(GROUPS):
        total = dkv[grp, seq].astype(F32)
        for i in range(PEERS - 1):
            total = total + kin[grp, i].astype(F32)
        dkv_out[:, grp * HEAD:(grp + 1) * HEAD] = total[:, 0:HEAD]
        dkv_out[:, 256 + grp * HEAD:256 + (grp + 1) * HEAD] = total[:, HEAD:256]
    for p in (1, 2, 0):
        first, wide = PARTS[p]
        for k in (1, 2, 3):
            third[p, k].wait_recv()
        full = b3[p][spots[p][2]].astype(F32)
        for k in range(3):
            full = full + r3[p][k].astype(F32)
        wg[:, first:first + wide] = full[0:SHARE] * (1.0 / math.sqrt(TOKENS))
    for c in started:
        c.wait_send()


def tree_call(pq, pk, pv, lq, lk, lv, pdy, ldy, w, lengths, offsets, parents):
    any_ = pl.BlockSpec(memory_space=pl.ANY)
    vm = pl.BlockSpec(memory_space=VMEM)
    sm = pl.BlockSpec(memory_space=SMEM)
    widths = [wide for _, wide in PARTS]
    dma = pltpu.SemaphoreType.DMA
    scratch = [
        pltpu.VMEM((PEERS, ROWS, 512), BF16),
        pltpu.VMEM((ROWS, D), BF16),
        pltpu.VMEM((ROWS, D), BF16),
        pltpu.VMEM((WIDTH // 256, 256, D), BF16),
        pltpu.VMEM((HEADS, ROWS, HEAD), BF16),
        pltpu.VMEM((HEADS, ROWS, HEAD), BF16),
        pltpu.VMEM((HEADS, ROWS, HEAD), BF16),
        pltpu.VMEM((HEADS, ROWS, KEYS), BF16),
        pltpu.VMEM((PER_KV, ROWS, KEYS), BF16),
        pltpu.VMEM((WIDTH, ROWS), F32),
        pltpu.VMEM((2, 4 * CHUNK, ROWS), F32),
        pltpu.VMEM((3, 2, 4, CHUNK, ROWS), BF16),
        pltpu.VMEM((3, 4, CHUNK, ROWS), BF16),
        pltpu.VMEM((ROWS, KEYS), F32),
        pltpu.VMEM((GROUPS, PEERS, ROWS, 256), BF16),
        pltpu.VMEM((GROUPS, PEERS - 1, ROWS, 256), BF16),
    ]
    scratch += [pltpu.VMEM((CHUNK, wide), F32) for wide in widths]
    scratch += [pltpu.VMEM((2, CHUNK, wide // 2), BF16) for wide in widths]
    scratch += [pltpu.VMEM((2, CHUNK, wide), BF16) for wide in widths]
    scratch += [pltpu.VMEM((4, 64, wide), BF16) for wide in widths]
    scratch += [pltpu.VMEM((3, 64, wide), BF16) for wide in widths]
    scratch += [pltpu.VMEM((4, 16, wide), BF16) for wide in widths]
    scratch += [pltpu.VMEM((3, 16, wide), BF16) for wide in widths]
    scratch += [dma((4,)), dma((2,)), dma((WIDTH // 256,)), dma((HEADS, 2)), dma((8,)), dma((8,))]
    scratch += [dma((2,)), dma((2,)), dma((3,)), dma((3,))]
    scratch += [dma((GROUPS, PEERS - 1)), dma((GROUPS, PEERS - 1)), dma((3, 6)), dma((3, 6))]
    scratch += [dma((3, 3)), dma((3, 3)), dma((3, 3)), dma((3, 3))]
    return pl.pallas_call(
        tree_kernel,
        out_shape=(
            jax.ShapeDtypeStruct((PROMPT, WIDTH), F32),
            jax.ShapeDtypeStruct((LEAF, WIDTH), F32),
            jax.ShapeDtypeStruct((SHARE, D), F32),
            jax.ShapeDtypeStruct((ROWS, 512), F32),
        ),
        in_specs=[any_] * 9 + [sm] * 3,
        out_specs=(vm,) * 4,
        scratch_shapes=scratch,
        compiler_params=pltpu.CompilerParams(
            collective_id=0, has_side_effects=True, vmem_limit_bytes=LIMIT
        ),
        name="tree",
    )(pq, pk, pv, lq, lk, lv, pdy, ldy, w, lengths, offsets, parents)


def finish_kernel(dqp, dql, wg, dkv, pdq, pdk, pdv, ldq, ldk, ldv, out):
    pdq[...] = dqp[...]
    ldq[...] = dql[...]
    pdk[...] = dkv[0:PROMPT, 0:256]
    pdv[...] = dkv[0:PROMPT, 256:512]
    ldk[...] = dkv[PROMPT:ROWS, 0:256]
    ldv[...] = dkv[PROMPT:ROWS, 256:512]
    out[...] = wg[...]


def finish_call(dqp, dql, wg, dkv):
    vm = pl.BlockSpec(memory_space=VMEM)
    return pl.pallas_call(
        finish_kernel,
        out_shape=(
            jax.ShapeDtypeStruct((PROMPT, WIDTH), F32),
            jax.ShapeDtypeStruct((PROMPT, 256), F32),
            jax.ShapeDtypeStruct((PROMPT, 256), F32),
            jax.ShapeDtypeStruct((LEAF, WIDTH), F32),
            jax.ShapeDtypeStruct((LEAF, 256), F32),
            jax.ShapeDtypeStruct((LEAF, 256), F32),
            jax.ShapeDtypeStruct((SHARE, D), F32),
        ),
        in_specs=[vm] * 4,
        out_specs=(vm,) * 7,
        name="finish",
    )(dqp, dql, wg, dkv)


def body(pq, pk, pv, lq, lk, lv, pdy, ldy, w, lengths, offsets, parents):
    done = tree_call(
        pq[0], pk[0], pv[0], lq[0], lk[0], lv[0], pdy[0], ldy[0], w, lengths, offsets, parents
    )
    outs = finish_call(*done)
    return tuple(o[None] for o in outs[0:6]) + (outs[6],)


def solution(mesh):
    rows = P("leaf", "seq", None)
    placed = (rows,) * 8 + (P(),) + (P("leaf", None),) * 3
    return jax.shard_map(
        body,
        mesh=mesh,
        in_specs=placed,
        out_specs=(rows,) * 6 + (P(("leaf", "seq"), None),),
        check_vma=False,
    )
```

time: 122 us -> 90.3 us (0.74)
  the two profiles are of different devices: /device:TPU:0 before, /device:TPU:1 now
where the time goes in v2:
time: 90.3 us; the launch traced here: 90.2 us
  Pallas kernels  89.5 us (99%)
    pallas_call x1, Pallas kernels, tree_call(): pl.pallas_call(tree_kernel, out_shape=(jax.ShapeDtypeStruct((PROMPT, WIDT...  86.8 us
    pallas_call x1, Pallas kernels, finish_call(): pl.pallas_call(finish_kernel, out_shape=(jax.ShapeDtypeStruct((PROMPT, WI...  2.68 us

profile of v2, /device:TPU:1, one launch (start us, length us, event | category | flops | bytes accessed | tf_op | source)
XLA Modules:
  0.0 90.2 jit_solution(17874111086717400900)
XLA Ops:
  0.6 86.8 %tree.1 = (f32[128,1792]{1,0:T(8,128)}, f32[48,1792]{1,0:T(8,128)}, f32[14,3584]{1,0:T(8,128)}, f32[176,512]{1,0:T(8,128)}) custom-call(bf16[128,1792]{1,0:T(8,128)(2,1)} %bitcast.15, bf16[128,256]{1,0:T(8,128)(2,1)} %bitcast.18, bf16[128,256]{1,0:T(8,128)(2,1)} %bitcast.19, bf16[48,1792]{1,0:T(8,128)(2,1)} %bitcast.17, bf16[48,256]{1,0:T(8,128)(2,1)} %bitcast.20, ...), custom_call_target="tpu_custom_call" | custom-call | tf_op jit(solution)/shard_map/tree/pallas_call | solution.py:431
  87.5 2.7 %finish.1 = (f32[128,1792]{1,0:T(8,128)}, f32[128,256]{1,0:T(8,128)}, f32[128,256]{1,0:T(8,128)}, f32[48,1792]{1,0:T(8,128)}, f32[48,256]{1,0:T(8,128)}, /*index=5*/f32[48,256]{1,0:T(8,128)}, f32[14,3584]{1,0:T(8,128)}) custom-call(f32[128,1792]{1,0:T(8,128)} %get-tuple-element.18.dqp, f32[48,1792]{1,0:T(8,128)} %get-tuple-element.19.dql, ...), custom_call_target="tpu_custom_call" | custom-call | tf_op jit(solution)/shard_map/finish/pallas_call | solution.py:461

commit v3 on v2

--- a/solution.py
+++ b/solution.py
@@ -26,7 +26,8 @@
 SCALE = 1.0 / math.sqrt(HEAD)
 LOG2E = 1.0 / math.log(2.0)
 NEG = -1e30
-PARTS = ((0, 1536), (1536, 1024), (2560, 1024))
+GATHERED = 2048
+PARTS = ((0, 1024), (1024, 1024), (2048, 768), (2816, 768))
 VMEM = pltpu.MemorySpace.VMEM
 SMEM = pltpu.MemorySpace.SMEM
 HALF = 256
@@ -113,16 +114,16 @@
     pq, pk, pv, lq, lk, lv, pdy, ldy, w, lengths, offsets, parents,
     dqp, dql, wg, dkv_out, *scratch
 ):
-    (kv, yo, yt, wbuf, g, qs, attn, ws, ds, at, perm, atp, ap, bias, dkv, kin) = scratch[0:16]
-    own = scratch[16:19]
-    rel = scratch[19:22]
-    rin = scratch[22:25]
-    b2 = scratch[25:28]
-    r2 = scratch[28:31]
-    b3 = scratch[31:34]
-    r3 = scratch[34:37]
-    (lsem, dsem, wsem, qsem, gsend, grecv, ysend, yrecv, asend, arecv,
-     ksend, krecv, s1, v1, s2, v2, s3, v3) = scratch[37:]
+    (kv, yo, yt, wbuf, g, qs, attn, ws, ds, at, perm, atn, atp, ap, ag, yg, bias, dkv, kin, sa, sb) = scratch[0:21]
+    own = dict(zip((2, 3), scratch[21:23]))
+    rel = dict(zip((2, 3), scratch[23:25]))
+    rin = dict(zip((2, 3), scratch[25:27]))
+    b2 = scratch[27:31]
+    r2 = scratch[31:35]
+    b3 = scratch[35:39]
+    r3 = scratch[39:43]
+    (lsem, dsem, wsem, qsem, gsend, grecv, ysend, yrecv, psend, precv, esend, erecv, asend, arecv,
+     ksend, krecv, s1, v1, s2, v2, s3, v3) = scratch[43:]
     leaf = lax.axis_index("leaf")
     seq = lax.axis_index("seq")
     core = leaf % 2
@@ -147,8 +148,11 @@
         return (y * 4 + (other // 2) * 2 + core, (other % 2) * 4 + x)
 
     across = (leaf, slot(1 - plane, 0))
-    axes = ((on_y, on_z, on_x), (on_x, on_y, on_z), (on_z, on_x, on_y))
-    spots = ((y, z, x), (x, y, z), (z, x, y))
+    def on_y_core(k, c):
+        return (((y + k) % 4) * 4 + ((leaf // 2) % 2) * 2 + c, seq)
+
+    axes = ((on_y, on_z, on_x), (on_y, on_x, on_z), (on_x, on_y, on_z), (on_z, on_y, on_x))
+    spots = ((y, z, x), (y, x, z), (x, y, z), (z, y, x))
 
     mine = [
         pltpu.make_async_copy(pk, kv.at[seq, 0:PROMPT, 0:256], lsem.at[0]),
@@ -177,6 +181,7 @@
     barrier = pltpu.get_barrier_semaphore()
     greet = [(leaf, p) for p in peers] + [twin]
     greet += [on_y(k) for k in (1, 2, 3)] + [on_z(k) for k in (1, 2, 3)]
+    greet += [on_y_core(k, 1 - core) for k in (1, 2, 3)]
     for d in greet:
         pl.semaphore_signal(barrier, inc=1, device_id=d, device_id_type=MESH)
     pl.semaphore_wait(barrier, len(greet))
@@ -206,6 +211,16 @@
     ]
     for c in ups:
         c.wait()
+
+    def strip(src, dst, i, device):
+        return go(src, dst, psend.at[i], precv.at[i], device)
+
+    def came(dst, i):
+        send_to(dst, dst, psend.at[i], precv.at[i], twin).wait_recv()
+
+    quarter = GATHERED // 2
+    strip(yo.at[:, 0:GATHERED], yg.at[2, core], 0, on_y(1))
+    strip(yo.at[:, 0:GATHERED], yg.at[0, core], 1, on_y(3))
 
     def tile(t, carry):
         pltpu.make_async_copy(w.at[0:256], wbuf.at[t], wsem.at[t]).wait()
@@ -240,39 +255,67 @@
         cols = pl.ds(pl.multiple_of(256 + grp * HEAD, HEAD), HEAD)
         return kv[:, :, cols].reshape(KEYS, HEAD)
 
-    def forward(h, carry):
-        grp = h // PER_KV
-        s = nt(qs[h], keys_of(grp)) * (SCALE * LOG2E) + bias[...]
-        top = jnp.max(s, axis=1, keepdims=True)
-        e = jnp.exp2(s - top)
-        total = jnp.sum(e, axis=1, keepdims=True)
-        weight = (e / total).astype(BF16)
-        ws[h] = weight
-        a = nn(weight, values_of(grp)).astype(BF16)
+    def score(h, out):
+        out[...] = nt(qs[h], keys_of(h // PER_KV))
+
+    def soften(h, src):
+        for r in range(0, ROWS, 16):
+            here = slice(r, r + 16)
+            t = src[here] * (SCALE * LOG2E) + bias[here]
+            e = jnp.exp2(t - jnp.max(t, axis=1, keepdims=True))
+            share = 1.0 / jnp.sum(e, axis=1, keepdims=True)
+            ws[h, here] = (e * share).astype(BF16)
+
+    def attend(h):
+        a = nn(ws[h], values_of(h // PER_KV)).astype(BF16)
         attn[h] = a
         at[pl.ds(pl.multiple_of(h * HEAD, HEAD), HEAD), :] = a.astype(F32).T
+
+    def forward(i, carry):
+        score(2 * i + 1, sb)
+        soften(2 * i, sa)
+        score(jnp.minimum(2 * i + 2, HEADS - 1), sa)
+        attend(2 * i)
+        soften(2 * i + 1, sb)
+        attend(2 * i + 1)
         return carry
 
-    lax.fori_loop(0, HEADS, forward, 0)
+    score(0, sa)
+    lax.fori_loop(0, 4, forward, 0)
+    came(yg.at[2, core], 0)
+    strip(yg.at[2, core, :, 0:quarter], yg.at[1, core, :, 0:quarter], 2, on_y(1))
+    came(yg.at[0, core], 1)
+    strip(yg.at[0, core, :, quarter:GATHERED], yg.at[1, core, :, quarter:GATHERED], 3, on_y(3))
+    strip(yg.at[2, core], yg.at[2, core], 4, twin)
+    strip(yg.at[0, core], yg.at[0, core], 5, twin)
+    lax.fori_loop(4, HEADS // 2, forward, 0)
     for c in range(2):
         for yy in range(4):
             for zh in range(2):
                 n = yy * 448 + zh * 224 + c * 112
-                atp[0, c, yy, zh * 112:(zh + 1) * 112, :] = at[n:n + 112, :].astype(BF16)
-        for xx in range(4):
-            for yy in range(4):
-                for zz in range(4):
-                    n = yy * 448 + (zz // 2) * 224 + c * 112 + (zz % 2) * 56 + xx * SHARE
+                atn[c, yy, zh * 112:(zh + 1) * 112, :] = at[n:n + 112, :].astype(BF16)
+    for k in (2, 1, 3):
+        for c in range(2):
+            go(atn.at[c, (y + k) % 4], ag.at[4 - k, core], esend.at[k, c], erecv.at[4 - k, core], on_y_core(k, c))
+    go(atn.at[1 - core, y], ag.at[0, core], esend.at[0, 0], erecv.at[0, core], twin)
+    for c in range(2):
+        for yy in range(4):
+            for zz in range(4):
+                n = yy * 448 + (zz // 2) * 224 + c * 112 + (zz % 2) * 56
+                r = zz * CHUNK + yy * 56
+                perm[1, r:r + 56, :] = at[n:n + 56, :]
+                for xx in range(4):
                     r = xx * CHUNK + yy * 56 + zz * SHARE
-                    perm[0, r:r + SHARE, :] = at[n:n + SHARE, :]
-                    r = zz * CHUNK + xx * 56 + yy * SHARE
-                    perm[1, r:r + SHARE, :] = at[n:n + SHARE, :]
+                    perm[0, r:r + SHARE, :] = at[n + xx * SHARE:n + (xx + 1) * SHARE, :]
         for k in range(4):
-            atp[1, c, k] = perm[0, k * CHUNK:(k + 1) * CHUNK, :].astype(BF16)
-            atp[2, c, k] = perm[1, k * CHUNK:(k + 1) * CHUNK, :].astype(BF16)
+            atp[0, c, k] = perm[0, k * CHUNK:(k + 1) * CHUNK, :].astype(BF16)
+            atp[1, c, k] = perm[1, k * CHUNK:(k + 1) * CHUNK, :].astype(BF16)
     rows = []
-    for p in range(3):
+    for p in range(2):
         rows.append(go(atp.at[p, 1 - core], ap.at[p], asend.at[p], arecv.at[p], twin))
+    came(yg.at[1, core, :, 0:quarter], 2)
+    came(yg.at[1, core, :, quarter:GATHERED], 3)
+    strip(yg.at[1, core], yg.at[1, core], 6, twin)
     for c in swaps:
         c.wait_recv()
     for c in rows:
@@ -286,24 +329,24 @@
         first, wide = PARTS[p]
         dest = (spots[p][0] + k) % 4
         cols = slice(first, first + wide)
-        return nn(atp[p, core, dest], yo[:, cols]) + nn(ap[p, dest], yt[:, cols])
+        return nn(atp[p - 2, core, dest], yo[:, cols]) + nn(ap[p - 2, dest], yt[:, cols])
 
     relays = {}
     direct = {}
-    for p in range(3):
+    for p in (2, 3):
         wide = PARTS[p][1]
         h = wide // 2
         part(p, 2, 0, wide)[...] = product(p, 2).astype(BF16)
-        relays[p, 0] = go(part(p, 2, 0, h), rel[p].at[0], s1.at[p, 0], v1.at[p, 0], axes[p][0](1))
-        relays[p, 1] = go(part(p, 2, h, wide), rel[p].at[1], s1.at[p, 1], v1.at[p, 1], axes[p][0](3))
-    for p in range(3):
+        relays[p, 0] = go(part(p, 2, 0, h), rel[p].at[0], s1.at[p - 2, 0], v1.at[p - 2, 0], axes[p][0](1))
+        relays[p, 1] = go(part(p, 2, h, wide), rel[p].at[1], s1.at[p - 2, 1], v1.at[p - 2, 1], axes[p][0](3))
+    for p in (2, 3):
         wide = PARTS[p][1]
         h = wide // 2
         part(p, 1, 0, wide)[...] = product(p, 1).astype(BF16)
-        direct[p, 0] = go(part(p, 1, h, wide), rin[p].at[0, :, h:wide], s1.at[p, 2], v1.at[p, 2], axes[p][0](1))
+        direct[p, 0] = go(part(p, 1, h, wide), rin[p].at[0, :, h:wide], s1.at[p - 2, 2], v1.at[p - 2, 2], axes[p][0](1))
         part(p, 3, 0, wide)[...] = product(p, 3).astype(BF16)
-        direct[p, 1] = go(part(p, 3, 0, h), rin[p].at[1, :, 0:h], s1.at[p, 3], v1.at[p, 3], axes[p][0](3))
-    for p in range(3):
+        direct[p, 1] = go(part(p, 3, 0, h), rin[p].at[1, :, 0:h], s1.at[p - 2, 3], v1.at[p - 2, 3], axes[p][0](3))
+    for p in (2, 3):
         own[p][...] = product(p, 0)
 
     def relay(p):
@@ -312,55 +355,119 @@
         relays[p, 0].wait_recv()
         here = part(p, 1, 0, h)
         here[...] = (here[...].astype(F32) + rel[p][0].astype(F32)).astype(BF16)
-        direct[p, 2] = go(here, rin[p].at[0, :, 0:h], s1.at[p, 4], v1.at[p, 4], axes[p][0](1))
+        direct[p, 2] = go(here, rin[p].at[0, :, 0:h], s1.at[p - 2, 4], v1.at[p - 2, 4], axes[p][0](1))
         relays[p, 1].wait_recv()
         here = part(p, 3, h, wide)
         here[...] = (here[...].astype(F32) + rel[p][1].astype(F32)).astype(BF16)
-        direct[p, 3] = go(here, rin[p].at[1, :, h:wide], s1.at[p, 5], v1.at[p, 5], axes[p][0](3))
-
-    grads = []
-    for grp in range(GROUPS):
-
+        direct[p, 3] = go(here, rin[p].at[1, :, h:wide], s1.at[p - 2, 5], v1.at[p - 2, 5], axes[p][0](3))
+
+    def heads_back(grp):
         def backward(j, carry):
             h = grp * PER_KV + j
             gh = g[h]
             dot = jnp.sum(gh.astype(F32) * attn[h].astype(F32), axis=1, keepdims=True)
             dp = nt(gh, values_of(grp))
-            dsc = (ws[h].astype(F32) * ((dp - dot) * SCALE)).astype(BF16)
+            dsc = (ws[h].astype(F32) * (dp - dot)).astype(BF16)
             ds[j] = dsc
-            dq = nn(dsc, keys_of(grp))
+            dq = nn(dsc, keys_of(grp)) * SCALE
             cols = pl.ds(pl.multiple_of(h * HEAD, HEAD), HEAD)
             dqp[:, cols] = dq[0:PROMPT]
             dql[:, cols] = dq[PROMPT:ROWS]
             return carry
 
         lax.fori_loop(0, PER_KV, backward, 0)
+
+    def keys_back(grp):
         stack = slice(grp * PER_KV, (grp + 1) * PER_KV)
         tall = PER_KV * ROWS
-        dk = tn(qs[stack].reshape(tall, HEAD), ds[...].reshape(tall, KEYS))
+        dk = tn(qs[stack].reshape(tall, HEAD), ds[...].reshape(tall, KEYS)) * SCALE
         dkv[grp, :, :, 0:HEAD] = dk.T.astype(BF16).reshape(PEERS, ROWS, HEAD)
         dv = tn(g[stack].reshape(tall, HEAD), ws[stack].reshape(tall, KEYS))
         dkv[grp, :, :, HEAD:256] = dv.T.astype(BF16).reshape(PEERS, ROWS, HEAD)
-        if grp == 0:
-            for p in (1, 2, 0):
-                relay(p)
-        for i, q in enumerate(peers):
-            grads.append(go(dkv.at[grp, q], kin.at[grp, i], ksend.at[grp, i], krecv.at[grp, i], (leaf, q)))
+
+    def hop(grp, i, src, dst, device):
+        return go(src, dst, ksend.at[grp, i], krecv.at[grp, i], device)
+
+    hops = {}
+
+    def add_in(grp, q, cols, i):
+        here = dkv.at[grp, q, :, cols]
+        here[...] = (here[...].astype(F32) + kin[grp, i, :, cols].astype(F32)).astype(BF16)
+
+    left, right, whole = slice(0, HEAD), slice(HEAD, 256), slice(0, 256)
+
+    def grads_one(grp):
+        hops[grp, 0] = hop(grp, 0, dkv.at[grp, slot(1 - plane, 2)], kin.at[grp, 0], across)
+        hops[grp, 1] = hop(grp, 1, dkv.at[grp, slot(1 - plane, 1)], kin.at[grp, 1], on_x(1))
+        hops[grp, 2] = hop(grp, 2, dkv.at[grp, slot(1 - plane, 3)], kin.at[grp, 2], on_x(3))
+
+    def grads_two(grp):
+        hops[grp, 0].wait_recv()
+        far = slot(plane, 2)
+        add_in(grp, far, whole, 0)
+        hops[grp, 3] = hop(grp, 3, dkv.at[grp, far, :, left], kin.at[grp, 3, :, left], on_x(1))
+        hops[grp, 4] = hop(grp, 4, dkv.at[grp, far, :, right], kin.at[grp, 3, :, right], on_x(3))
+        hops[grp, 1].wait_recv()
+        hops[grp, 2].wait_recv()
+        near = slot(1 - plane, 0)
+        total = dkv[grp, near].astype(F32) + kin[grp, 1].astype(F32) + kin[grp, 2].astype(F32)
+        dkv[grp, near] = total.astype(BF16)
+        hops[grp, 7] = hop(grp, 7, dkv.at[grp, near], kin.at[grp, 4], across)
+
+    def grads_three(grp):
+        hops[grp, 3].wait_recv()
+        add_in(grp, slot(plane, 1), left, 3)
+        hops[grp, 5] = hop(grp, 5, dkv.at[grp, slot(plane, 1)], kin.at[grp, 5], on_x(1))
+        hops[grp, 4].wait_recv()
+        add_in(grp, slot(plane, 3), right, 3)
+        hops[grp, 6] = hop(grp, 6, dkv.at[grp, slot(plane, 3)], kin.at[grp, 6], on_x(3))
+
+    def grads_last(grp):
+        total = dkv[grp, seq].astype(F32)
+        for i in (7, 5, 6):
+            hops[grp, i].wait_recv()
+        for i in (4, 5, 6):
+            total = total + kin[grp, i].astype(F32)
+        dkv_out[:, grp * HEAD:(grp + 1) * HEAD] = total[:, 0:HEAD]
+        dkv_out[:, 256 + grp * HEAD:256 + (grp + 1) * HEAD] = total[:, HEAD:256]
+
     second = {}
-    for p in (1, 2, 0):
-        wide = PARTS[p][1]
-        for i in range(4):
-            direct[p, i].wait_recv()
-        pad = jnp.zeros((8, wide), F32)
+    third = {}
+
+    def send_second(p, pieces):
+        pad = jnp.zeros((8, PARTS[p][1]), F32)
         for j in range(4):
-            piece = slice(j * 56, (j + 1) * 56)
-            full = own[p][piece] + rin[p][0, piece].astype(F32) + rin[p][1, piece].astype(F32)
-            b2[p][j] = jnp.concatenate([full, pad], axis=0).astype(BF16)
+            b2[p][j] = jnp.concatenate([pieces[j], pad], axis=0).astype(BF16)
         spot = spots[p][1]
         for k in (2, 1, 3):
             second[p, k] = go(b2[p].at[(spot + k) % 4], r2[p].at[k - 1], s2.at[p, k - 1], v2.at[p, k - 1], axes[p][1](k))
-    third = {}
-    for p in (1, 2, 0):
+
+    def gathered(p):
+        first, wide = PARTS[p]
+        cols = slice(first, first + wide)
+        full = nn(atn[core, y], yo[:, cols]) + nn(ag[0, 1 - core], yt[:, cols])
+        for k in (1, 3, 2):
+            for c in range(2):
+                full = full + nn(ag[k, c], yg[k - 1, c, :, cols])
+        if p == 0:
+            send_second(p, [full[j * 56:(j + 1) * 56] for j in range(4)])
+        else:
+            strips = []
+            for j in range(4):
+                rows_of = [full[zz * 56 + j * SHARE:zz * 56 + (j + 1) * SHARE] for zz in range(4)]
+                strips.append(jnp.concatenate(rows_of, axis=0))
+            send_second(p, strips)
+
+    def scattered(p):
+        for i in range(4):
+            direct[p, i].wait_recv()
+        pieces = []
+        for j in range(4):
+            piece = slice(j * 56, (j + 1) * 56)
+            pieces.append(own[p][piece] + rin[p][0, piece].astype(F32) + rin[p][1, piece].astype(F32))
+        send_second(p, pieces)
+
+    def send_third(p):
         for k in (1, 2, 3):
             second[p, k].wait_recv()
         full = b2[p][spots[p][1]].astype(F32)
@@ -373,15 +480,36 @@
         spot = spots[p][2]
         for k in (2, 1, 3):
             third[p, k] = go(b3[p].at[(spot + k) % 4], r3[p].at[k - 1], s3.at[p, k - 1], v3.at[p, k - 1], axes[p][2](k))
-    for c in grads:
-        c.wait_recv()
-    for grp in range(GROUPS):
-        total = dkv[grp, seq].astype(F32)
-        for i in range(PEERS - 1):
-            total = total + kin[grp, i].astype(F32)
-        dkv_out[:, grp * HEAD:(grp + 1) * HEAD] = total[:, 0:HEAD]
-        dkv_out[:, 256 + grp * HEAD:256 + (grp + 1) * HEAD] = total[:, HEAD:256]
-    for p in (1, 2, 0):
+
+    heads_back(0)
+    relay(2)
+    relay(3)
+    keys_back(0)
+    grads_one(0)
+    send_to(ag.at[0, 1 - core], ag.at[0, 1 - core], esend.at[0, 0], erecv.at[0, 1 - core], twin).wait_recv()
+    for k in (1, 2, 3):
+        for c in range(2):
+            send_to(ag.at[k, c], ag.at[k, c], esend.at[k, c], erecv.at[k, c], twin).wait_recv()
+    came(yg.at[2, 1 - core], 4)
+    came(yg.at[0, 1 - core], 5)
+    came(yg.at[1, 1 - core], 6)
+    gathered(0)
+    gathered(1)
+    heads_back(1)
+    scattered(2)
+    scattered(3)
+    keys_back(1)
+    grads_one(1)
+    grads_two(0)
+    send_third(0)
+    send_third(1)
+    grads_two(1)
+    grads_three(0)
+    send_third(2)
+    send_third(3)
+    grads_three(1)
+    grads_last(0)
+    for p in range(4):
         first, wide = PARTS[p]
         for k in (1, 2, 3):
             third[p, k].wait_recv()
@@ -389,6 +517,7 @@
         for k in range(3):
             full = full + r3[p][k].astype(F32)
         wg[:, first:first + wide] = full[0:SHARE] * (1.0 / math.sqrt(TOKENS))
+    grads_last(1)
     for c in started:
         c.wait_send()
 
@@ -411,23 +540,29 @@
         pltpu.VMEM((PER_KV, ROWS, KEYS), BF16),
         pltpu.VMEM((WIDTH, ROWS), F32),
         pltpu.VMEM((2, 4 * CHUNK, ROWS), F32),
-        pltpu.VMEM((3, 2, 4, CHUNK, ROWS), BF16),
-        pltpu.VMEM((3, 4, CHUNK, ROWS), BF16),
+        pltpu.VMEM((2, 4, CHUNK, ROWS), BF16),
+        pltpu.VMEM((2, 2, 4, CHUNK, ROWS), BF16),
+        pltpu.VMEM((2, 4, CHUNK, ROWS), BF16),
+        pltpu.VMEM((4, 2, CHUNK, ROWS), BF16),
+        pltpu.VMEM((3, 2, ROWS, GATHERED), BF16),
         pltpu.VMEM((ROWS, KEYS), F32),
         pltpu.VMEM((GROUPS, PEERS, ROWS, 256), BF16),
-        pltpu.VMEM((GROUPS, PEERS - 1, ROWS, 256), BF16),
+        pltpu.VMEM((GROUPS, 7, ROWS, 256), BF16),
+        pltpu.VMEM((ROWS, KEYS), F32),
+        pltpu.VMEM((ROWS, KEYS), F32),
     ]
-    scratch += [pltpu.VMEM((CHUNK, wide), F32) for wide in widths]
-    scratch += [pltpu.VMEM((2, CHUNK, wide // 2), BF16) for wide in widths]
-    scratch += [pltpu.VMEM((2, CHUNK, wide), BF16) for wide in widths]
+    late = widths[2:]
+    scratch += [pltpu.VMEM((CHUNK, wide), F32) for wide in late]
+    scratch += [pltpu.VMEM((2, CHUNK, wide // 2), BF16) for wide in late]
+    scratch += [pltpu.VMEM((2, CHUNK, wide), BF16) for wide in late]
     scratch += [pltpu.VMEM((4, 64, wide), BF16) for wide in widths]
     scratch += [pltpu.VMEM((3, 64, wide), BF16) for wide in widths]
     scratch += [pltpu.VMEM((4, 16, wide), BF16) for wide in widths]
     scratch += [pltpu.VMEM((3, 16, wide), BF16) for wide in widths]
     scratch += [dma((4,)), dma((2,)), dma((WIDTH // 256,)), dma((HEADS, 2)), dma((8,)), dma((8,))]
-    scratch += [dma((2,)), dma((2,)), dma((3,)), dma((3,))]
-    scratch += [dma((GROUPS, PEERS - 1)), dma((GROUPS, PEERS - 1)), dma((3, 6)), dma((3, 6))]
-    scratch += [dma((3, 3)), dma((3, 3)), dma((3, 3)), dma((3, 3))]
+    scratch += [dma((2,)), dma((2,)), dma((7,)), dma((7,)), dma((4, 2)), dma((4, 2)), dma((2,)), dma((2,))]
+    scratch += [dma((GROUPS, 8)), dma((GROUPS, 8)), dma((2, 6)), dma((2, 6))]
+    scratch += [dma((4, 3)), dma((4, 3)), dma((4, 3)), dma((4, 3))]
     return pl.pallas_call(
         tree_kernel,
         out_shape=(

time: 90.3 us -> 78.5 us (0.87)
  the two profiles are of different devices: /device:TPU:1 before, /device:TPU:0 now
where the time goes in v3:
time: 78.5 us; the launch traced here: 78.3 us
  Pallas kernels  77.7 us (99%)
    pallas_call x1, Pallas kernels, tree_call(): pl.pallas_call(tree_kernel, out_shape=(jax.ShapeDtypeStruct((PROMPT, WIDT...  75 us
    pallas_call x1, Pallas kernels, finish_call(): pl.pallas_call(finish_kernel, out_shape=(jax.ShapeDtypeStruct((PROMPT, WI...  2.68 us

profile of v3, /device:TPU:0, one launch (start us, length us, event | category | flops | bytes accessed | tf_op | source)
XLA Modules:
  0.0 78.3 jit_solution(7607337580244385882)
XLA Ops:
  0.6 75.0 %tree.1 = (f32[128,1792]{1,0:T(8,128)}, f32[48,1792]{1,0:T(8,128)}, f32[14,3584]{1,0:T(8,128)}, f32[176,512]{1,0:T(8,128)}) custom-call(bf16[128,1792]{1,0:T(8,128)(2,1)} %bitcast.15, bf16[128,256]{1,0:T(8,128)(2,1)} %bitcast.18, bf16[128,256]{1,0:T(8,128)(2,1)} %bitcast.19, bf16[48,1792]{1,0:T(8,128)(2,1)} %bitcast.17, bf16[48,256]{1,0:T(8,128)(2,1)} %bitcast.20, ...), custom_call_target="tpu_custom_call" | custom-call | tf_op jit(solution)/shard_map/tree/pallas_call | solution.py:566
  75.6 2.7 %finish.1 = (f32[128,1792]{1,0:T(8,128)}, f32[128,256]{1,0:T(8,128)}, f32[128,256]{1,0:T(8,128)}, f32[48,1792]{1,0:T(8,128)}, f32[48,256]{1,0:T(8,128)}, /*index=5*/f32[48,256]{1,0:T(8,128)}, f32[14,3584]{1,0:T(8,128)}) custom-call(f32[128,1792]{1,0:T(8,128)} %get-tuple-element.18.dqp, f32[48,1792]{1,0:T(8,128)} %get-tuple-element.19.dql, ...), custom_call_target="tpu_custom_call" | custom-call | tf_op jit(solution)/shard_map/finish/pallas_call | solution.py:596

commit v4 on v3

--- a/solution.py
+++ b/solution.py
@@ -203,8 +203,10 @@
         c.wait()
     block = kv.at[seq]
     pass_on(block, 0, across)
-    pass_on(block, 1, on_x(1))
-    pass_on(block, 2, on_x(3))
+    pass_on(kv.at[seq, :, 0:HALF], 1, on_x(1))
+    pass_on(kv.at[seq, :, HALF:512], 2, on_x(3))
+    pass_on(kv.at[seq, :, HALF:512], 8, on_x(1))
+    pass_on(kv.at[seq, :, 0:HALF], 9, on_x(3))
     swaps = [
         go(pdy, yt.at[0:PROMPT], ysend.at[0], yrecv.at[0], twin),
         go(ldy, yt.at[PROMPT:ROWS], ysend.at[1], yrecv.at[1], twin),
@@ -219,8 +221,11 @@
         send_to(dst, dst, psend.at[i], precv.at[i], twin).wait_recv()
 
     quarter = GATHERED // 2
-    strip(yo.at[:, 0:GATHERED], yg.at[2, core], 0, on_y(1))
-    strip(yo.at[:, 0:GATHERED], yg.at[0, core], 1, on_y(3))
+    lower, upper = slice(0, quarter), slice(quarter, GATHERED)
+    strip(yo.at[:, lower], yg.at[2, core, :, lower], 0, on_y(1))
+    strip(yo.at[:, upper], yg.at[0, core, :, upper], 1, on_y(3))
+    strip(yo.at[:, upper], yg.at[2, core, :, upper], 2, on_y(1))
+    strip(yo.at[:, lower], yg.at[0, core, :, lower], 3, on_y(3))
 
     def tile(t, carry):
         pltpu.make_async_copy(w.at[0:256], wbuf.at[t], wsem.at[t]).wait()
@@ -230,9 +235,9 @@
         return carry
 
     lax.fori_loop(0, tiles, tile, 0)
-    arrived(kv.at[slot(plane, 3)], 1)
+    arrived(kv.at[slot(plane, 3), :, 0:HALF], 1)
     pass_on(kv.at[slot(plane, 3), :, 0:HALF], 3, on_x(1))
-    arrived(kv.at[slot(plane, 1)], 2)
+    arrived(kv.at[slot(plane, 1), :, HALF:512], 2)
     pass_on(kv.at[slot(plane, 1), :, HALF:512], 4, on_x(3))
     arrived(kv.at[slot(1 - plane, 0)], 0)
     pass_on(kv.at[slot(1 - plane, 0)], 5, on_x(1))
@@ -243,6 +248,12 @@
     pass_on(kv.at[slot(plane, 2)], 7, across)
     for c in queries:
         c.wait()
+    came(yg.at[2, core, :, lower], 0)
+    strip(yg.at[2, core, :, lower], yg.at[1, core, :, lower], 4, on_y(1))
+    came(yg.at[0, core, :, upper], 1)
+    strip(yg.at[0, core, :, upper], yg.at[1, core, :, upper], 5, on_y(3))
+    arrived(kv.at[slot(plane, 3), :, HALF:512], 8)
+    arrived(kv.at[slot(plane, 1), :, 0:HALF], 9)
     arrived(kv.at[slot(1 - plane, 3)], 5)
     arrived(kv.at[slot(1 - plane, 1)], 6)
     arrived(kv.at[slot(1 - plane, 2)], 7)
@@ -282,12 +293,10 @@
 
     score(0, sa)
     lax.fori_loop(0, 4, forward, 0)
-    came(yg.at[2, core], 0)
-    strip(yg.at[2, core, :, 0:quarter], yg.at[1, core, :, 0:quarter], 2, on_y(1))
-    came(yg.at[0, core], 1)
-    strip(yg.at[0, core, :, quarter:GATHERED], yg.at[1, core, :, quarter:GATHERED], 3, on_y(3))
-    strip(yg.at[2, core], yg.at[2, core], 4, twin)
-    strip(yg.at[0, core], yg.at[0, core], 5, twin)
+    came(yg.at[2, core, :, upper], 2)
+    strip(yg.at[2, core], yg.at[2, core], 6, twin)
+    came(yg.at[0, core, :, lower], 3)
+    strip(yg.at[0, core], yg.at[0, core], 7, twin)
     lax.fori_loop(4, HEADS // 2, forward, 0)
     for c in range(2):
         for yy in range(4):
@@ -313,13 +322,6 @@
     rows = []
     for p in range(2):
         rows.append(go(atp.at[p, 1 - core], ap.at[p], asend.at[p], arecv.at[p], twin))
-    came(yg.at[1, core, :, 0:quarter], 2)
-    came(yg.at[1, core, :, quarter:GATHERED], 3)
-    strip(yg.at[1, core], yg.at[1, core], 6, twin)
-    for c in swaps:
-        c.wait_recv()
-    for c in rows:
-        c.wait_recv()
 
     def part(p, k, lo, hi):
         first = PARTS[p][0]
@@ -333,6 +335,144 @@
 
     relays = {}
     direct = {}
+
+    def relay(p):
+        wide = PARTS[p][1]
+        h = wide // 2
+        relays[p, 0].wait_recv()
+        here = part(p, 1, 0, h)
+        here[...] = (here[...].astype(F32) + rel[p][0].astype(F32)).astype(BF16)
+        direct[p, 2] = go(here, rin[p].at[0, :, 0:h], s1.at[p - 2, 4], v1.at[p - 2, 4], axes[p][0](1))
+        relays[p, 1].wait_recv()
+        here = part(p, 3, h, wide)
+        here[...] = (here[...].astype(F32) + rel[p][1].astype(F32)).astype(BF16)
+        direct[p, 3] = go(here, rin[p].at[1, :, h:wide], s1.at[p - 2, 5], v1.at[p - 2, 5], axes[p][0](3))
+
+    def heads_back(grp, first=0, last=PER_KV):
+        def backward(j, carry):
+            h = grp * PER_KV + j
+            gh = g[h]
+            dot = jnp.sum(gh.astype(F32) * attn[h].astype(F32), axis=1, keepdims=True)
+            dp = nt(gh, values_of(grp))
+            dsc = (ws[h].astype(F32) * (dp - dot)).astype(BF16)
+            ds[j] = dsc
+            dq = nn(dsc, keys_of(grp)) * SCALE
+            cols = pl.ds(pl.multiple_of(h * HEAD, HEAD), HEAD)
+            dqp[:, cols] = dq[0:PROMPT]
+            dql[:, cols] = dq[PROMPT:ROWS]
+            return carry
+
+        lax.fori_loop(first, last, backward, 0)
+
+    def keys_back(grp):
+        stack = slice(grp * PER_KV, (grp + 1) * PER_KV)
+        tall = PER_KV * ROWS
+        dk = tn(qs[stack].reshape(tall, HEAD), ds[...].reshape(tall, KEYS)) * SCALE
+        dkv[grp, :, :, 0:HEAD] = dk.T.astype(BF16).reshape(PEERS, ROWS, HEAD)
+        dv = tn(g[stack].reshape(tall, HEAD), ws[stack].reshape(tall, KEYS))
+        dkv[grp, :, :, HEAD:256] = dv.T.astype(BF16).reshape(PEERS, ROWS, HEAD)
+
+    def hop(grp, i, src, dst, device):
+        return go(src, dst, ksend.at[grp, i], krecv.at[grp, i], device)
+
+    hops = {}
+
+    def add_in(grp, q, cols, i):
+        here = dkv.at[grp, q, :, cols]
+        here[...] = (here[...].astype(F32) + kin[grp, i, :, cols].astype(F32)).astype(BF16)
+
+    left, right, whole = slice(0, HEAD), slice(HEAD, 256), slice(0, 256)
+
+    def grads_one(grp):
+        hops[grp, 0] = hop(grp, 0, dkv.at[grp, slot(1 - plane, 2)], kin.at[grp, 0], across)
+        hops[grp, 1] = hop(grp, 1, dkv.at[grp, slot(1 - plane, 1)], kin.at[grp, 1], on_x(1))
+        hops[grp, 2] = hop(grp, 2, dkv.at[grp, slot(1 - plane, 3)], kin.at[grp, 2], on_x(3))
+
+    def grads_two(grp):
+        hops[grp, 0].wait_recv()
+        far = slot(plane, 2)
+        add_in(grp, far, whole, 0)
+        hops[grp, 3] = hop(grp, 3, dkv.at[grp, far, :, left], kin.at[grp, 3, :, left], on_x(1))
+        hops[grp, 4] = hop(grp, 4, dkv.at[grp, far, :, right], kin.at[grp, 3, :, right], on_x(3))
+        hops[grp, 1].wait_recv()
+        hops[grp, 2].wait_recv()
+        near = slot(1 - plane, 0)
+        total = dkv[grp, near].astype(F32) + kin[grp, 1].astype(F32) + kin[grp, 2].astype(F32)
+        dkv[grp, near] = total.astype(BF16)
+        hops[grp, 7] = hop(grp, 7, dkv.at[grp, near], kin.at[grp, 4], across)
+
+    def grads_three(grp):
+        hops[grp, 3].wait_recv()
+        add_in(grp, slot(plane, 1), left, 3)
+        hops[grp, 5] = hop(grp, 5, dkv.at[grp, slot(plane, 1)], kin.at[grp, 5], on_x(1))
+        hops[grp, 4].wait_recv()
+        add_in(grp, slot(plane, 3), right, 3)
+        hops[grp, 6] = hop(grp, 6, dkv.at[grp, slot(plane, 3)], kin.at[grp, 6], on_x(3))
+
+    def grads_last(grp):
+        total = dkv[grp, seq].astype(F32)
+        for i in (7, 5, 6):
+            hops[grp, i].wait_recv()
+        for i in (4, 5, 6):
+            total = total + kin[grp, i].astype(F32)
+        dkv_out[:, grp * HEAD:(grp + 1) * HEAD] = total[:, 0:HEAD]
+        dkv_out[:, 256 + grp * HEAD:256 + (grp + 1) * HEAD] = total[:, HEAD:256]
+
+    second = {}
+    third = {}
+
+    def send_second(p, pieces):
+        pad = jnp.zeros((8, PARTS[p][1]), F32)
+        for j in range(4):
+            b2[p][j] = jnp.concatenate([pieces[j], pad], axis=0).astype(BF16)
+        spot = spots[p][1]
+        for k in (2, 1, 3):
+            second[p, k] = go(b2[p].at[(spot + k) % 4], r2[p].at[k - 1], s2.at[p, k - 1], v2.at[p, k - 1], axes[p][1](k))
+
+    def gathered(p):
+        first, wide = PARTS[p]
+        cols = slice(first, first + wide)
+        full = nn(atn[core, y], yo[:, cols]) + nn(ag[0, 1 - core], yt[:, cols])
+        for k in (1, 3, 2):
+            for c in range(2):
+                full = full + nn(ag[k, c], yg[k - 1, c, :, cols])
+        if p == 0:
+            send_second(p, [full[j * 56:(j + 1) * 56] for j in range(4)])
+        else:
+            strips = []
+            for j in range(4):
+                rows_of = [full[zz * 56 + j * SHARE:zz * 56 + (j + 1) * SHARE] for zz in range(4)]
+                strips.append(jnp.concatenate(rows_of, axis=0))
+            send_second(p, strips)
+
+    def scattered(p):
+        for i in range(4):
+            direct[p, i].wait_recv()
+        pieces = []
+        for j in range(4):
+            piece = slice(j * 56, (j + 1) * 56)
+            pieces.append(own[p][piece] + rin[p][0, piece].astype(F32) + rin[p][1, piece].astype(F32))
+        send_second(p, pieces)
+
+    def send_third(p):
+        for k in (1, 2, 3):
+            second[p, k].wait_recv()
+        full = b2[p][spots[p][1]].astype(F32)
+        for k in range(3):
+            full = full + r2[p][k].astype(F32)
+        pad = jnp.zeros((2, PARTS[p][1]), F32)
+        for j in range(4):
+            piece = full[j * SHARE:(j + 1) * SHARE]
+            b3[p][j] = jnp.concatenate([piece, pad], axis=0).astype(BF16)
+        spot = spots[p][2]
+        for k in (2, 1, 3):
+            third[p, k] = go(b3[p].at[(spot + k) % 4], r3[p].at[k - 1], s3.at[p, k - 1], v3.at[p, k - 1], axes[p][2](k))
+
+    heads_back(0, 0, 3)
+    for c in swaps:
+        c.wait_recv()
+    for c in rows:
+        c.wait_recv()
     for p in (2, 3):
         wide = PARTS[p][1]
         h = wide // 2
@@ -348,166 +488,36 @@
         direct[p, 1] = go(part(p, 3, 0, h), rin[p].at[1, :, 0:h], s1.at[p - 2, 3], v1.at[p - 2, 3], axes[p][0](3))
     for p in (2, 3):
         own[p][...] = product(p, 0)
-
-    def relay(p):
-        wide = PARTS[p][1]
-        h = wide // 2
-        relays[p, 0].wait_recv()
-        here = part(p, 1, 0, h)
-        here[...] = (here[...].astype(F32) + rel[p][0].astype(F32)).astype(BF16)
-        direct[p, 2] = go(here, rin[p].at[0, :, 0:h], s1.at[p - 2, 4], v1.at[p - 2, 4], axes[p][0](1))
-        relays[p, 1].wait_recv()
-        here = part(p, 3, h, wide)
-        here[...] = (here[...].astype(F32) + rel[p][1].astype(F32)).astype(BF16)
-        direct[p, 3] = go(here, rin[p].at[1, :, h:wide], s1.at[p - 2, 5], v1.at[p - 2, 5], axes[p][0](3))
-
-    def heads_back(grp):
-        def backward(j, carry):
-            h = grp * PER_KV + j
-            gh = g[h]
-            dot = jnp.sum(gh.astype(F32) * attn[h].astype(F32), axis=1, keepdims=True)
-            dp = nt(gh, values_of(grp))
-            dsc = (ws[h].astype(F32) * (dp - dot)).astype(BF16)
-            ds[j] = dsc
-            dq = nn(dsc, keys_of(grp)) * SCALE
-            cols = pl.ds(pl.multiple_of(h * HEAD, HEAD), HEAD)
-            dqp[:, cols] = dq[0:PROMPT]
-            dql[:, cols] = dq[PROMPT:ROWS]
-            return carry
-
-        lax.fori_loop(0, PER_KV, backward, 0)
-
-    def keys_back(grp):
-        stack = slice(grp * PER_KV, (grp + 1) * PER_KV)
-        tall = PER_KV * ROWS
-        dk = tn(qs[stack].reshape(tall, HEAD), ds[...].reshape(tall, KEYS)) * SCALE
-        dkv[grp, :, :, 0:HEAD] = dk.T.astype(BF16).reshape(PEERS, ROWS, HEAD)
-        dv = tn(g[stack].reshape(tall, HEAD), ws[stack].reshape(tall, KEYS))
-        dkv[grp, :, :, HEAD:256] = dv.T.astype(BF16).reshape(PEERS, ROWS, HEAD)
-
-    def hop(grp, i, src, dst, device):
-        return go(src, dst, ksend.at[grp, i], krecv.at[grp, i], device)
-
-    hops = {}
-
-    def add_in(grp, q, cols, i):
-        here = dkv.at[grp, q, :, cols]
-        here[...] = (here[...].astype(F32) + kin[grp, i, :, cols].astype(F32)).astype(BF16)
-
-    left, right, whole = slice(0, HEAD), slice(HEAD, 256), slice(0, 256)
-
-    def grads_one(grp):
-        hops[grp, 0] = hop(grp, 0, dkv.at[grp, slot(1 - plane, 2)], kin.at[grp, 0], across)
-        hops[grp, 1] = hop(grp, 1, dkv.at[grp, slot(1 - plane, 1)], kin.at[grp, 1], on_x(1))
-        hops[grp, 2] = hop(grp, 2, dkv.at[grp, slot(1 - plane, 3)], kin.at[grp, 2], on_x(3))
-
-    def grads_two(grp):
-        hops[grp, 0].wait_recv()
-        far = slot(plane, 2)
-        add_in(grp, far, whole, 0)
-        hops[grp, 3] = hop(grp, 3, dkv.at[grp, far, :, left], kin.at[grp, 3, :, left], on_x(1))
-        hops[grp, 4] = hop(grp, 4, dkv.at[grp, far, :, right], kin.at[grp, 3, :, right], on_x(3))
-        hops[grp, 1].wait_recv()
-        hops[grp, 2].wait_recv()
-        near = slot(1 - plane, 0)
-        total = dkv[grp, near].astype(F32) + kin[grp, 1].astype(F32) + kin[grp, 2].astype(F32)
-        dkv[grp, near] = total.astype(BF16)
-        hops[grp, 7] = hop(grp, 7, dkv.at[grp, near], kin.at[grp, 4], across)
-
-    def grads_three(grp):
-        hops[grp, 3].wait_recv()
-        add_in(grp, slot(plane, 1), left, 3)
-        hops[grp, 5] = hop(grp, 5, dkv.at[grp, slot(plane, 1)], kin.at[grp, 5], on_x(1))
-        hops[grp, 4].wait_recv()
-        add_in(grp, slot(plane, 3), right, 3)
-        hops[grp, 6] = hop(grp, 6, dkv.at[grp, slot(plane, 3)], kin.at[grp, 6], on_x(3))
-
-    def grads_last(grp):
-        total = dkv[grp, seq].astype(F32)
-        for i in (7, 5, 6):
-            hops[grp, i].wait_recv()
-        for i in (4, 5, 6):
-            total = total + kin[grp, i].astype(F32)
-        dkv_out[:, grp * HEAD:(grp + 1) * HEAD] = total[:, 0:HEAD]
-        dkv_out[:, 256 + grp * HEAD:256 + (grp + 1) * HEAD] = total[:, HEAD:256]
-
-    second = {}
-    third = {}
-
-    def send_second(p, pieces):
-        pad = jnp.zeros((8, PARTS[p][1]), F32)
-        for j in range(4):
-            b2[p][j] = jnp.concatenate([pieces[j], pad], axis=0).astype(BF16)
-        spot = spots[p][1]
-        for k in (2, 1, 3):
-            second[p, k] = go(b2[p].at[(spot + k) % 4], r2[p].at[k - 1], s2.at[p, k - 1], v2.at[p, k - 1], axes[p][1](k))
-
-    def gathered(p):
-        first, wide = PARTS[p]
-        cols = slice(first, first + wide)
-        full = nn(atn[core, y], yo[:, cols]) + nn(ag[0, 1 - core], yt[:, cols])
-        for k in (1, 3, 2):
-            for c in range(2):
-                full = full + nn(ag[k, c], yg[k - 1, c, :, cols])
-        if p == 0:
-            send_second(p, [full[j * 56:(j + 1) * 56] for j in range(4)])
-        else:
-            strips = []
-            for j in range(4):
-                rows_of = [full[zz * 56 + j * SHARE:zz * 56 + (j + 1) * SHARE] for zz in range(4)]
-                strips.append(jnp.concatenate(rows_of, axis=0))
-            send_second(p, strips)
-
-    def scattered(p):
-        for i in range(4):
-            direct[p, i].wait_recv()
-        pieces = []
-        for j in range(4):
-            piece = slice(j * 56, (j + 1) * 56)
-            pieces.append(own[p][piece] + rin[p][0, piece].astype(F32) + rin[p][1, piece].astype(F32))
-        send_second(p, pieces)
-
-    def send_third(p):
-        for k in (1, 2, 3):
-            second[p, k].wait_recv()
-        full = b2[p][spots[p][1]].astype(F32)
-        for k in range(3):
-            full = full + r2[p][k].astype(F32)
-        pad = jnp.zeros((2, PARTS[p][1]), F32)
-        for j in range(4):
-            piece = full[j * SHARE:(j + 1) * SHARE]
-            b3[p][j] = jnp.concatenate([piece, pad], axis=0).astype(BF16)
-        spot = spots[p][2]
-        for k in (2, 1, 3):
-            third[p, k] = go(b3[p].at[(spot + k) % 4], r3[p].at[k - 1], s3.at[p, k - 1], v3.at[p, k - 1], axes[p][2](k))
-
-    heads_back(0)
+    heads_back(0, 3, PER_KV)
+    keys_back(0)
+    grads_one(0)
+    came(yg.at[1, core, :, lower], 4)
+    came(yg.at[1, core, :, upper], 5)
+    strip(yg.at[1, core], yg.at[1, core], 8, twin)
     relay(2)
     relay(3)
-    keys_back(0)
-    grads_one(0)
+    heads_back(1)
     send_to(ag.at[0, 1 - core], ag.at[0, 1 - core], esend.at[0, 0], erecv.at[0, 1 - core], twin).wait_recv()
     for k in (1, 2, 3):
         for c in range(2):
             send_to(ag.at[k, c], ag.at[k, c], esend.at[k, c], erecv.at[k, c], twin).wait_recv()
-    came(yg.at[2, 1 - core], 4)
-    came(yg.at[0, 1 - core], 5)
-    came(yg.at[1, 1 - core], 6)
+    came(yg.at[2, 1 - core], 6)
+    came(yg.at[0, 1 - core], 7)
+    came(yg.at[1, 1 - core], 8)
     gathered(0)
     gathered(1)
-    heads_back(1)
-    scattered(2)
-    scattered(3)
     keys_back(1)
     grads_one(1)
     grads_two(0)
+    scattered(2)
+    scattered(3)
+    grads_two(1)
+    grads_three(0)
     send_third(0)
     send_third(1)
-    grads_two(1)
-    grads_three(0)
+    grads_three(1)
     send_third(2)
     send_third(3)
-    grads_three(1)
     grads_last(0)
     for p in range(4):
         first, wide = PARTS[p]
@@ -559,8 +569,8 @@
     scratch += [pltpu.VMEM((3, 64, wide), BF16) for wide in widths]
     scratch += [pltpu.VMEM((4, 16, wide), BF16) for wide in widths]
     scratch += [pltpu.VMEM((3, 16, wide), BF16) for wide in widths]
-    scratch += [dma((4,)), dma((2,)), dma((WIDTH // 256,)), dma((HEADS, 2)), dma((8,)), dma((8,))]
-    scratch += [dma((2,)), dma((2,)), dma((7,)), dma((7,)), dma((4, 2)), dma((4, 2)), dma((2,)), dma((2,))]
+    scratch += [dma((4,)), dma((2,)), dma((WIDTH // 256,)), dma((HEADS, 2)), dma((10,)), dma((10,))]
+    scratch += [dma((2,)), dma((2,)), dma((9,)), dma((9,)), dma((4, 2)), dma((4, 2)), dma((2,)), dma((2,))]
     scratch += [dma((GROUPS, 8)), dma((GROUPS, 8)), dma((2, 6)), dma((2, 6))]
     scratch += [dma((4, 3)), dma((4, 3)), dma((4, 3)), dma((4, 3))]
     return pl.pallas_call(

time: 78.5 us -> 75.3 us (0.959)
  Pallas kernels: 77.7 us -> 74 us
    pallas_call x1, Pallas kernels: 75 us -> 71.3 us  [tree_call(): pl.pallas_call(tree_kernel, out_shape=(jax.ShapeDtypeStruct((PROMPT, WIDT...]
where the time goes in v4:
time: 75.3 us; the launch traced here: 74.7 us
  Pallas kernels  74 us (98%)
    pallas_call x1, Pallas kernels, tree_call(): pl.pallas_call(tree_kernel, out_shape=(jax.ShapeDtypeStruct((PROMPT, WIDT...  71.3 us
    pallas_call x1, Pallas kernels, finish_call(): pl.pallas_call(finish_kernel, out_shape=(jax.ShapeDtypeStruct((PROMPT, WI...  2.68 us

profile of v4, /device:TPU:0, one launch (start us, length us, event | category | flops | bytes accessed | tf_op | source)
XLA Modules:
  0.0 74.7 jit_solution(14510274499577658135)
XLA Ops:
  0.6 71.3 %tree.1 = (f32[128,1792]{1,0:T(8,128)}, f32[48,1792]{1,0:T(8,128)}, f32[14,3584]{1,0:T(8,128)}, f32[176,512]{1,0:T(8,128)}) custom-call(bf16[128,1792]{1,0:T(8,128)(2,1)} %bitcast.15, bf16[128,256]{1,0:T(8,128)(2,1)} %bitcast.18, bf16[128,256]{1,0:T(8,128)(2,1)} %bitcast.19, bf16[48,1792]{1,0:T(8,128)(2,1)} %bitcast.17, bf16[48,256]{1,0:T(8,128)(2,1)} %bitcast.20, ...), custom_call_target="tpu_custom_call" | custom-call | tf_op jit(solution)/shard_map/tree/pallas_call | solution.py:576
  72.0 2.7 %finish.1 = (f32[128,1792]{1,0:T(8,128)}, f32[128,256]{1,0:T(8,128)}, f32[128,256]{1,0:T(8,128)}, f32[48,1792]{1,0:T(8,128)}, f32[48,256]{1,0:T(8,128)}, /*index=5*/f32[48,256]{1,0:T(8,128)}, f32[14,3584]{1,0:T(8,128)}) custom-call(f32[128,1792]{1,0:T(8,128)} %get-tuple-element.18.dqp, f32[48,1792]{1,0:T(8,128)} %get-tuple-element.19.dql, ...), custom_call_target="tpu_custom_call" | custom-call | tf_op jit(solution)/shard_map/finish/pallas_call | solution.py:606

commit v5 on v4

--- a/solution.py
+++ b/solution.py
@@ -26,6 +26,7 @@
 SCALE = 1.0 / math.sqrt(HEAD)
 LOG2E = 1.0 / math.log(2.0)
 NEG = -1e30
+HALF_ROWS = CHUNK // 2
 GATHERED = 2048
 PARTS = ((0, 1024), (1024, 1024), (2048, 768), (2816, 768))
 VMEM = pltpu.MemorySpace.VMEM
@@ -112,7 +113,7 @@
 
 def tree_kernel(
     pq, pk, pv, lq, lk, lv, pdy, ldy, w, lengths, offsets, parents,
-    dqp, dql, wg, dkv_out, *scratch
+    dqp_out, dql_out, wg, dkv_out, *scratch
 ):
     (kv, yo, yt, wbuf, g, qs, attn, ws, ds, at, perm, atn, atp, ap, ag, yg, bias, dkv, kin, sa, sb) = scratch[0:21]
     own = dict(zip((2, 3), scratch[21:23]))
@@ -123,7 +124,7 @@
     b3 = scratch[35:39]
     r3 = scratch[39:43]
     (lsem, dsem, wsem, qsem, gsend, grecv, ysend, yrecv, psend, precv, esend, erecv, asend, arecv,
-     ksend, krecv, s1, v1, s2, v2, s3, v3) = scratch[43:]
+     ksend, krecv, s1, v1, s2, v2, s3, v3, dqp, dql, osem) = scratch[43:]
     leaf = lax.axis_index("leaf")
     seq = lax.axis_index("seq")
     core = leaf % 2
@@ -266,6 +267,78 @@
         cols = pl.ds(pl.multiple_of(256 + grp * HEAD, HEAD), HEAD)
         return kv[:, :, cols].reshape(KEYS, HEAD)
 
+    def part(p, k, u, lo, hi):
+        first = PARTS[p][0]
+        return wbuf.at[k, HALF_ROWS * u:HALF_ROWS * (u + 1), first + lo:first + hi]
+
+    def strips_of(u):
+        return slice(HALF_ROWS * u, HALF_ROWS * (u + 1))
+
+    def product(p, k, u):
+        first, wide = PARTS[p]
+        dest = (spots[p][0] + k) % 4
+        cols = slice(first, first + wide)
+        here = strips_of(u)
+        return nn(atp[p - 2, core, dest, here], yo[:, cols]) + nn(ap[p - 2, dest, here], yt[:, cols])
+
+    relays = {}
+    direct = {}
+    rows = {}
+
+    def arrange(u):
+        here = strips_of(u)
+        for c in range(2):
+            for yy in (2 * u, 2 * u + 1):
+                for zz in range(4):
+                    n = yy * 448 + (zz // 2) * 224 + c * 112 + (zz % 2) * 56
+                    r = zz * CHUNK + yy * 56
+                    perm[1, r:r + 56, :] = at[n:n + 56, :]
+                    for xx in range(4):
+                        r = xx * CHUNK + yy * 56 + zz * SHARE
+                        perm[0, r:r + SHARE, :] = at[n + xx * SHARE:n + (xx + 1) * SHARE, :]
+            for k in range(4):
+                for p in range(2):
+                    r = k * CHUNK + u * HALF_ROWS
+                    atp[p, c, k, here] = perm[p, r:r + HALF_ROWS, :].astype(BF16)
+        for p in range(2):
+            rows[p, u] = go(atp.at[p, 1 - core, :, here], ap.at[p, :, here], asend.at[p, u], arecv.at[p, u], twin)
+
+    def multiply(u):
+        here = strips_of(u)
+        for p in range(2):
+            rows[p, u].wait_recv()
+        for p in (2, 3):
+            wide = PARTS[p][1]
+            h = wide // 2
+            n = p - 2
+            part(p, 2, u, 0, wide)[...] = product(p, 2, u).astype(BF16)
+            relays[p, u, 0] = go(part(p, 2, u, 0, h), rel[p].at[0, here], s1.at[n, u, 0], v1.at[n, u, 0], axes[p][0](1))
+            relays[p, u, 1] = go(part(p, 2, u, h, wide), rel[p].at[1, here], s1.at[n, u, 1], v1.at[n, u, 1], axes[p][0](3))
+        for p in (2, 3):
+            wide = PARTS[p][1]
+            h = wide // 2
+            n = p - 2
+            part(p, 1, u, 0, wide)[...] = product(p, 1, u).astype(BF16)
+            direct[p, u, 0] = go(part(p, 1, u, h, wide), rin[p].at[0, here, h:wide], s1.at[n, u, 2], v1.at[n, u, 2], axes[p][0](1))
+            part(p, 3, u, 0, wide)[...] = product(p, 3, u).astype(BF16)
+            direct[p, u, 1] = go(part(p, 3, u, 0, h), rin[p].at[1, here, 0:h], s1.at[n, u, 3], v1.at[n, u, 3], axes[p][0](3))
+        for p in (2, 3):
+            own[p][here] = product(p, 0, u)
+
+    def relay(p, u):
+        wide = PARTS[p][1]
+        h = wide // 2
+        n = p - 2
+        rows_of = strips_of(u)
+        relays[p, u, 0].wait_recv()
+        here = part(p, 1, u, 0, h)
+        here[...] = (here[...].astype(F32) + rel[p][0, rows_of].astype(F32)).astype(BF16)
+        direct[p, u, 2] = go(here, rin[p].at[0, rows_of, 0:h], s1.at[n, u, 4], v1.at[n, u, 4], axes[p][0](1))
+        relays[p, u, 1].wait_recv()
+        here = part(p, 3, u, h, wide)
+        here[...] = (here[...].astype(F32) + rel[p][1, rows_of].astype(F32)).astype(BF16)
+        direct[p, u, 3] = go(here, rin[p].at[1, rows_of, h:wide], s1.at[n, u, 5], v1.at[n, u, 5], axes[p][0](3))
+
     def score(h, out):
         out[...] = nt(qs[h], keys_of(h // PER_KV))
 
@@ -297,7 +370,12 @@
     strip(yg.at[2, core], yg.at[2, core], 6, twin)
     came(yg.at[0, core, :, lower], 3)
     strip(yg.at[0, core], yg.at[0, core], 7, twin)
-    lax.fori_loop(4, HEADS // 2, forward, 0)
+    arrange(0)
+    lax.fori_loop(4, 6, forward, 0)
+    for c in swaps:
+        c.wait_recv()
+    multiply(0)
+    lax.fori_loop(6, HEADS // 2, forward, 0)
     for c in range(2):
         for yy in range(4):
             for zh in range(2):
@@ -307,47 +385,6 @@
         for c in range(2):
             go(atn.at[c, (y + k) % 4], ag.at[4 - k, core], esend.at[k, c], erecv.at[4 - k, core], on_y_core(k, c))
     go(atn.at[1 - core, y], ag.at[0, core], esend.at[0, 0], erecv.at[0, core], twin)
-    for c in range(2):
-        for yy in range(4):
-            for zz in range(4):
-                n = yy * 448 + (zz // 2) * 224 + c * 112 + (zz % 2) * 56
-                r = zz * CHUNK + yy * 56
-                perm[1, r:r + 56, :] = at[n:n + 56, :]
-                for xx in range(4):
-                    r = xx * CHUNK + yy * 56 + zz * SHARE
-                    perm[0, r:r + SHARE, :] = at[n + xx * SHARE:n + (xx + 1) * SHARE, :]
-        for k in range(4):
-            atp[0, c, k] = perm[0, k * CHUNK:(k + 1) * CHUNK, :].astype(BF16)
-            atp[1, c, k] = perm[1, k * CHUNK:(k + 1) * CHUNK, :].astype(BF16)
-    rows = []
-    for p in range(2):
-        rows.append(go(atp.at[p, 1 - core], ap.at[p], asend.at[p], arecv.at[p], twin))
-
-    def part(p, k, lo, hi):
-        first = PARTS[p][0]
-        return wbuf.at[k, 0:CHUNK, first + lo:first + hi]
-
-    def product(p, k):
-        first, wide = PARTS[p]
-        dest = (spots[p][0] + k) % 4
-        cols = slice(first, first + wide)
-        return nn(atp[p - 2, core, dest], yo[:, cols]) + nn(ap[p - 2, dest], yt[:, cols])
-
-    relays = {}
-    direct = {}
-
-    def relay(p):
-        wide = PARTS[p][1]
-        h = wide // 2
-        relays[p, 0].wait_recv()
-        here = part(p, 1, 0, h)
-        here[...] = (here[...].astype(F32) + rel[p][0].astype(F32)).astype(BF16)
-        direct[p, 2] = go(here, rin[p].at[0, :, 0:h], s1.at[p - 2, 4], v1.at[p - 2, 4], axes[p][0](1))
-        relays[p, 1].wait_recv()
-        here = part(p, 3, h, wide)
-        here[...] = (here[...].astype(F32) + rel[p][1].astype(F32)).astype(BF16)
-        direct[p, 3] = go(here, rin[p].at[1, :, h:wide], s1.at[p - 2, 5], v1.at[p - 2, 5], axes[p][0](3))
-
     def heads_back(grp, first=0, last=PER_KV):
         def backward(j, carry):
             h = grp * PER_KV + j
@@ -446,8 +483,9 @@
             send_second(p, strips)
 
     def scattered(p):
-        for i in range(4):
-            direct[p, i].wait_recv()
+        for u in range(2):
+            for i in range(4):
+                direct[p, u, i].wait_recv()
         pieces = []
         for j in range(4):
             piece = slice(j * 56, (j + 1) * 56)
@@ -468,35 +506,29 @@
         for k in (2, 1, 3):
             third[p, k] = go(b3[p].at[(spot + k) % 4], r3[p].at[k - 1], s3.at[p, k - 1], v3.at[p, k - 1], axes[p][2](k))
 
+    arrange(1)
     heads_back(0, 0, 3)
-    for c in swaps:
-        c.wait_recv()
-    for c in rows:
-        c.wait_recv()
-    for p in (2, 3):
-        wide = PARTS[p][1]
-        h = wide // 2
-        part(p, 2, 0, wide)[...] = product(p, 2).astype(BF16)
-        relays[p, 0] = go(part(p, 2, 0, h), rel[p].at[0], s1.at[p - 2, 0], v1.at[p - 2, 0], axes[p][0](1))
-        relays[p, 1] = go(part(p, 2, h, wide), rel[p].at[1], s1.at[p - 2, 1], v1.at[p - 2, 1], axes[p][0](3))
-    for p in (2, 3):
-        wide = PARTS[p][1]
-        h = wide // 2
-        part(p, 1, 0, wide)[...] = product(p, 1).astype(BF16)
-        direct[p, 0] = go(part(p, 1, h, wide), rin[p].at[0, :, h:wide], s1.at[p - 2, 2], v1.at[p - 2, 2], axes[p][0](1))
-        part(p, 3, 0, wide)[...] = product(p, 3).astype(BF16)
-        direct[p, 1] = go(part(p, 3, 0, h), rin[p].at[1, :, 0:h], s1.at[p - 2, 3], v1.at[p - 2, 3], axes[p][0](3))
-    for p in (2, 3):
-        own[p][...] = product(p, 0)
+    multiply(1)
+    relay(2, 0)
+    relay(3, 0)
     heads_back(0, 3, PER_KV)
     keys_back(0)
     grads_one(0)
+    relay(2, 1)
+    relay(3, 1)
     came(yg.at[1, core, :, lower], 4)
     came(yg.at[1, core, :, upper], 5)
     strip(yg.at[1, core], yg.at[1, core], 8, twin)
-    relay(2)
-    relay(3)
     heads_back(1)
+    outs = [
+        pltpu.make_async_copy(dqp, dqp_out, osem.at[0]),
+        pltpu.make_async_copy(dql, dql_out, osem.at[1]),
+    ]
+    for c in outs:
+        c.start()
+    keys_back(1)
+    grads_one(1)
+    grads_two(0)
     send_to(ag.at[0, 1 - core], ag.at[0, 1 - core], esend.at[0, 0], erecv.at[0, 1 - core], twin).wait_recv()
     for k in (1, 2, 3):
         for c in range(2):
@@ -506,19 +538,17 @@
     came(yg.at[1, 1 - core], 8)
     gathered(0)
     gathered(1)
-    keys_back(1)
-    grads_one(1)
-    grads_two(0)
+    grads_three(0)
+    grads_two(1)
     scattered(2)
     scattered(3)
-    grads_two(1)
-    grads_three(0)
+    grads_three(1)
     send_third(0)
     send_third(1)
-    grads_three(1)
+    grads_last(0)
     send_third(2)
     send_third(3)
-    grads_last(0)
+    grads_last(1)
     for p in range(4):
         first, wide = PARTS[p]
         for k in (1, 2, 3):
@@ -527,7 +557,8 @@
         for k in range(3):
             full = full + r3[p][k].astype(F32)
         wg[:, first:first + wide] = full[0:SHARE] * (1.0 / math.sqrt(TOKENS))
-    grads_last(1)
+    for c in outs:
+        c.wait()
     for c in started:
         c.wait_send()
 
@@ -570,9 +601,10 @@
     scratch += [pltpu.VMEM((4, 16, wide), BF16) for wide in widths]
     scratch += [pltpu.VMEM((3, 16, wide), BF16) for wide in widths]
     scratch += [dma((4,)), dma((2,)), dma((WIDTH // 256,)), dma((HEADS, 2)), dma((10,)), dma((10,))]
-    scratch += [dma((2,)), dma((2,)), dma((9,)), dma((9,)), dma((4, 2)), dma((4, 2)), dma((2,)), dma((2,))]
-    scratch += [dma((GROUPS, 8)), dma((GROUPS, 8)), dma((2, 6)), dma((2, 6))]
+    scratch += [dma((2,)), dma((2,)), dma((9,)), dma((9,)), dma((4, 2)), dma((4, 2)), dma((2, 2)), dma((2, 2))]
+    scratch += [dma((GROUPS, 8)), dma((GROUPS, 8)), dma((2, 2, 6)), dma((2, 2, 6))]
     scratch += [dma((4, 3)), dma((4, 3)), dma((4, 3)), dma((4, 3))]
+    scratch += [pltpu.VMEM((PROMPT, WIDTH), F32), pltpu.VMEM((LEAF, WIDTH), F32), dma((2,))]
     return pl.pallas_call(
         tree_kernel,
         out_shape=(
@@ -582,7 +614,7 @@
             jax.ShapeDtypeStruct((ROWS, 512), F32),
         ),
         in_specs=[any_] * 9 + [sm] * 3,
-        out_specs=(vm,) * 4,
+        out_specs=(any_, any_, vm, vm),
         scratch_shapes=scratch,
         compiler_params=pltpu.CompilerParams(
             collective_id=0, has_side_effects=True, vmem_limit_bytes=LIMIT

time: 75.3 us -> 75.1 us (level)
  no operation moved by 1% of the time
where the time goes in v5:
time: 75.1 us; the launch traced here: 75 us
  Pallas kernels  74.3 us (99%)
    pallas_call x1, Pallas kernels, tree_call(): pl.pallas_call(tree_kernel, out_shape=(jax.ShapeDtypeStruct((PROMPT, WIDT...  71.7 us
    pallas_call x1, Pallas kernels, finish_call(): pl.pallas_call(finish_kernel, out_shape=(jax.ShapeDtypeStruct((PROMPT, WI...  2.68 us

profile of v5, /device:TPU:0, one launch (start us, length us, event | category | flops | bytes accessed | tf_op | source)
XLA Modules:
  0.0 75.0 jit_solution(5269170169419650613)
XLA Ops:
  0.6 71.7 %tree.1 = (f32[128,1792]{1,0:T(8,128)}, f32[48,1792]{1,0:T(8,128)}, f32[14,3584]{1,0:T(8,128)}, f32[176,512]{1,0:T(8,128)}) custom-call(bf16[128,1792]{1,0:T(8,128)(2,1)} %bitcast.15, bf16[128,256]{1,0:T(8,128)(2,1)} %bitcast.18, bf16[128,256]{1,0:T(8,128)(2,1)} %bitcast.19, bf16[48,1792]{1,0:T(8,128)(2,1)} %bitcast.17, bf16[48,256]{1,0:T(8,128)(2,1)} %bitcast.20, ...), custom_call_target="tpu_custom_call" | custom-call | tf_op jit(solution)/shard_map/tree/pallas_call | solution.py:608
  72.3 2.7 %finish.1 = (f32[128,1792]{1,0:T(8,128)}, f32[128,256]{1,0:T(8,128)}, f32[128,256]{1,0:T(8,128)}, f32[48,1792]{1,0:T(8,128)}, f32[48,256]{1,0:T(8,128)}, /*index=5*/f32[48,256]{1,0:T(8,128)}, f32[14,3584]{1,0:T(8,128)}) custom-call(f32[128,1792]{1,0:T(8,128)} %get-tuple-element.18.dqp, f32[48,1792]{1,0:T(8,128)} %get-tuple-element.19.dql, ...), custom_call_target="tpu_custom_call" | custom-call | tf_op jit(solution)/shard_map/finish/pallas_call | solution.py:638
